TPU v7x, 256 devices: a whole 4x4x8 slice. The times are simulated.
256 devices in a mesh: gx: 4 (over y), gy: 16 (over z, x_lo), gz: 4 (over x_hi, core).
Axes of the slice: x: 4 (x_hi: 2, x_lo: 2; x = x_hi * 2 + x_lo), y: 4, z: 8, core: 2. Of those that a mesh axis runs over, the one named last changes fastest.
Arguments:
- features: bfloat16 [4, 16, 4, 128, 512], P('gx', 'gy', 'gz'), may hold values from -6 to 6
- positions: int32 [4, 16, 4, 3, 128], P('gx', 'gy', 'gz'), may hold values from 0 to 16383, as said below
- species: int32 [4, 16, 4, 128], P('gx', 'gy', 'gz'), may hold values from 0 to 9
- counts: int32 [4, 16, 4], P('gx', 'gy', 'gz'), may hold values from 64 to 128, as said below
- neighbors: int32 [4, 16, 4, 12, 128], P('gx', 'gy', 'gz'), may hold values from 0 to 3455, as said below
- waves: int32 [3, 2048], replicated, may hold values from -8 to 8, as said below
- radial_in: bfloat16 [8, 64], replicated, may hold values from -2 to 2
- radial_out: bfloat16 [64, 128], replicated, may hold values from -0.75 to 0.75
- species_gain: float32 [10, 128], replicated, may hold values from 0.5 to 1.5
- mix_weight: bfloat16 [128, 128], replicated, may hold values from -0.5 to 0.5
- readout: float32 [128], replicated, may hold values from -0.5 to 0.5
- charge_weight: float32 [128, 8], replicated, may hold values from -0.5 to 0.5
- ref_energy: float32 [10], replicated, may hold values from -4 to 4
Outputs:
- site_energy: float32 [4, 16, 4, 128], P('gx', 'gy', 'gz')
- forces: float32 [4, 16, 4, 3, 128], P('gx', 'gy', 'gz')
Inputs may be any that keep to these rules, and one draw needn't show every extreme that they name: The first counts[a, b, c] slots of a cell hold atoms, the others are empty. `positions`: an atom of global cell n has coordinate n * 1024 plus 0 to 1023 along each dimension. `neighbors`: entry ((a * 3 + b) * 3 + c) * 128 + s names slot s of cell (a, b, c) of the device's block extended by one cell on every side, counted from the extended block's corner; it is an occupied slot of one of the 27 cells around the atom's own cell. `waves`: the first component is 1 to 8, the others -8 to 8.
All inputs are finite; a program needn't handle non-finite values.
Results may differ from a plain program's by a relative error of at most 0.004.
Values may be sent and summed in bfloat16 or wider, within the bound.
A program may use at most 64 MiB of HBM per device.

v0:
```python
import functools
import math

import jax
import jax.numpy as jnp
from jax import lax
from jax.experimental import pallas as pl
from jax.experimental.pallas import tpu as pltpu
from jax.sharding import PartitionSpec as P

TICKS = 1024
AXES = ("gx", "gy", "gz")
MESH = pl.DeviceIdType.MESH
HIGH = lax.Precision.HIGHEST
OFFS = [(a - 1, b - 1, c - 1) for a in range(3) for b in range(3) for c in range(3)]
F32 = jnp.float32
BF16 = jnp.bfloat16
SLOT = 128
GROUP = 9
FAR = -1.0e6


def iota(shape, dim):
    return lax.broadcasted_iota(jnp.int32, shape, dim)


def dot(a, b, contract=((1,), (0,)), precision=None):
    return lax.dot_general(a, b, (contract, ((), ())), precision=precision, preferred_element_type=F32)


NT = ((1,), (1,))
TN = ((0,), (0,))


def split(x):
    hi = x.astype(BF16)
    return hi, (x - hi.astype(F32)).astype(BF16)


def at_offset(sizes, d):
    return tuple(lax.rem(lax.axis_index(n) + (s + o), s) if o else lax.axis_index(n) for n, s, o in zip(AXES, sizes, d))


def greet(sizes, offsets):
    barrier = pltpu.get_barrier_semaphore()
    for d in offsets:
        pl.semaphore_signal(barrier, inc=1, device_id=at_offset(sizes, d), device_id_type=MESH)
    return lambda: pl.semaphore_wait(barrier, len(offsets))


def send(src, dst, ssem, rsem, sizes, d):
    c = pltpu.make_async_remote_copy(
        src_ref=src, dst_ref=dst, send_sem=ssem, recv_sem=rsem, device_id=at_offset(sizes, d), device_id_type=MESH
    )
    c.start()
    return c


NEAR = [(i, d) for i, d in enumerate(OFFS) if d != (0, 0, 0)]


def spread_kernel(
    sizes, pack, feats, species, rin, rout, gain, mix, readout, cw, ref_energy,
    lists, gtab, mst, wz, wr, base9, refrow, ssem, rsem, csem,
):
    wait = greet(sizes, [d for _, d in NEAR])
    wait()
    copies = [send(pack, lists.at[26 - i], ssem.at[i], rsem.at[i], sizes, d) for i, d in NEAR]
    own = pltpu.make_async_copy(pack, lists.at[13], csem)
    own.start()
    neigh = 12
    lane = iota((8, SLOT), 1)
    sel8 = jnp.where(lax.rem(lane, 16) == iota((8, SLOT), 0), 1.0, 0.0)
    sel1 = jnp.where(lax.rem(iota((1, SLOT), 1), 16) == 8, 1.0, 0.0)
    rc = dot(cw[...], sel8, precision=HIGH) + dot(readout[...], sel1, TN, HIGH)
    m = dot(mix[...].astype(F32), rc, precision=HIGH) * (neigh ** -0.5)
    mhi, mlo = split(m)
    mst[0:128, :] = mhi
    mst[128:256, :] = mlo
    base9[...] = dot(rc, feats[...].astype(F32), ((0,), (1,)), HIGH)[0:16]
    kinds = gain.shape[0]
    onehot = jnp.where(iota((kinds, SLOT), 0) == species[...], 1.0, 0.0)
    ghi, glo = split(dot(onehot, gain[...], TN, HIGH))
    gtab[:, 0:128] = ghi
    gtab[:, 128:256] = glo
    refrow[...] = jnp.broadcast_to(dot(ref_energy[...], onehot, precision=HIGH), refrow.shape)
    r = rin[...]
    h = rin.shape[1]
    dup = jnp.where(lax.rem(iota((h, 128), 1), h) == iota((h, 128), 0), 1.0, 0.0).astype(BF16)
    upper = jnp.where(iota((h, 128), 1) - h == iota((h, 128), 0), 1.0, 0.0).astype(BF16)
    rows_a = jnp.where(iota((128, 8), 0) == iota((128, 8), 1), 1.0, 0.0).astype(BF16)
    rows_b = jnp.where(iota((128, 8), 0) - 8 == iota((128, 8), 1), 1.0, 0.0).astype(BF16)
    wz[:, 0:128] = dot(dot(rows_a, r).astype(BF16), dup).astype(BF16)
    wz[:, 128:256] = dot(dot(rows_b, r).astype(BF16), upper).astype(BF16)
    ro = rout[...]
    none = jnp.zeros_like(ro)
    wr[0:64, 0:128] = ro
    wr[64:128, 0:128] = none
    wr[0:64, 128:256] = none
    wr[64:128, 128:256] = ro
    for c in copies:
        c.wait()
    own.wait()


def rows_of(loc):
    hi = loc & ~31
    return hi.astype(F32).astype(BF16), (loc & 31).astype(F32).astype(BF16)


def edges(blk, rank, base, off, own, feats, gtab, mst, wz, wr):
    slot = iota((SLOT, 128), 0).astype(F32) + base
    code = ((blk & 127) + 1).astype(F32)
    acc = jnp.zeros((SLOT, 128), F32)
    for k in range(12):
        acc = jnp.where(rank[k : k + 1] == slot, code[k : k + 1], acc)
    accb = acc.astype(BF16)
    pick_i = jnp.where(acc > 0.0, 1.0, 0.0).astype(BF16)
    named = dot(accb, jnp.ones((128, 128), BF16))
    lane = iota((SLOT, 128), 1)
    pick_j = jnp.where(named == (lane + 1).astype(F32), 1.0, 0.0).astype(BF16)
    both = jnp.concatenate([pick_i, pick_j], axis=1)
    disp = []
    for d in range(3):
        ihi, ilo = rows_of(blk[12 + d : 13 + d] & (TICKS - 1))
        jhi, jlo = rows_of(own[d : d + 1] & (TICKS - 1))
        hi = jnp.concatenate([-ihi, jhi], axis=1)
        lo = jnp.concatenate([-ilo, jlo], axis=1)
        w = jnp.concatenate([jnp.broadcast_to(hi, (128, 256)), jnp.broadcast_to(lo, (128, 256))], axis=0)
        t = dot(both, w, NT)
        disp.append((t[:, 0:128] + t[:, 128:256]) * (1.0 / TICKS) - off[d])
    dx, dy, dz = disp
    r2 = dx * dx + dy * dy + dz * dz
    s2 = r2 + 0.25
    inv = lax.rsqrt(s2)
    rs = s2 * inv
    inv1 = 1.0 / (1.0 + r2)
    t = rs - (0.25 + 0.5 * lax.rem(lane, 8).astype(F32))
    b = jnp.exp(-2.0 * t * t) * inv1
    b = jnp.where(lane < 8, b, b * (-4.0 * t - 2.0 * rs * inv1)).astype(BF16)
    zz = dot(b, wz)
    z, zp = zz[:, 0:128], zz[:, 128:256]
    sig = 1.0 / (1.0 + jnp.exp(-z))
    silu = z * sig
    hid = jnp.where(lane < 64, silu, (sig + silu * (1.0 - sig)) * zp).astype(BF16)
    rr = dot(hid, wr)
    g = dot(pick_j, gtab)
    g = g[:, 0:128] + g[:, 128:256]
    rad = rr[:, 0:128] * g
    radp = rr[:, 128:256] * g
    h = dot(pick_j, feats)
    q, qp = [], []
    for d in range(4):
        hd = h[:, 128 * d : 128 * (d + 1)]
        x = (rad * hd).astype(BF16)
        q.append(dot(jnp.concatenate([x, x], axis=1), mst))
        x = (radp * hd).astype(BF16)
        qp.append(dot(jnp.concatenate([x, x], axis=1), mst))
    ux, uy, uz = dx * inv, dy * inv, dz * inv
    along = ux * q[1] + uy * q[2] + uz * q[3]
    w = qp[0] + ux * qp[1] + uy * qp[2] + uz * qp[3] - along * inv
    part = (lane >> 4) & 3
    ua = jnp.where(part == 0, ux, jnp.where(part == 1, uy, uz))
    qa = jnp.where(part == 0, q[1], jnp.where(part == 1, q[2], q[3]))
    out = jnp.where(part == 3, q[0] + along, ua * w + qa * inv)
    return pick_i, pick_j, out


def per_atom(pick_i, out):
    lane = iota((SLOT, 128), 1)
    hi = out.astype(BF16)
    mixed = jnp.where(lane < 64, hi.astype(F32), out - hi.astype(F32)).astype(BF16)
    s = dot(mixed, pick_i, TN)
    return s[0:64] + s[64:128]


def cell_offset(a):
    return ((a // 9 - 1).astype(F32), (lax.rem(a // 3, 3) - 1).astype(F32), (lax.rem(a, 3) - 1).astype(F32))


def edge_kernel(lists, pack, feats, gtab, mst, wz, wr, sums_t, sums_j, picks_i, picks_j, outs, ranks, most, mask):
    lane = iota((16, 128), 1)
    row = iota((16, 128), 0)
    for a in range(27):
        blk = lists[a]
        keep = ((blk >> 7) == 26 - a) & (lane < blk[15:16]) & (row < 12)
        mask[16 * a : 16 * a + 16] = jnp.where(keep, 1.0, 0.0)
    m = mask[...].astype(BF16)
    tri = jnp.where(iota((128, 128), 0) <= iota((128, 128), 1), 1.0, 0.0).astype(BF16)
    both = dot(m, jnp.concatenate([tri, jnp.ones((128, 128), BF16)], axis=1))
    lower = jnp.where(iota((16, 16), 0) > iota((16, 16), 1), 1.0, 0.0).astype(BF16)
    totals = jnp.concatenate([both[16 * a : 16 * a + 16, 128:256] for a in range(27)], axis=1).astype(BF16)
    start = dot(lower, totals)
    peak = start[12:16, 0:128]
    for a in range(27):
        s = start[:, 128 * a : 128 * a + 128]
        peak = jnp.maximum(peak, s[12:16])
        r = both[16 * a : 16 * a + 16, 0:128] + s - 1.0
        ranks[a] = jnp.where(mask[16 * a : 16 * a + 16] > 0.0, r, FAR)
    most[0:4] = peak
    most[4:8] = peak
    own = pack[12:15]

    def group(gi, carry):
        done = []
        for u in range(GROUP):
            a = gi * GROUP + u
            done.append((a, edges(lists[a], ranks[a], 0.0, cell_offset(a), own, feats[...], gtab[...], mst[...], wz[...], wr[...])))
        for a, (pick_i, pick_j, out) in done:
            picks_i[a] = pick_i
            picks_j[a] = pick_j
            outs[a] = out
            s = per_atom(pick_i, out)
            sums_j[a] = s[0:48]
            sums_t[a] = s[48:64]
        return carry

    lax.fori_loop(0, 27 // GROUP, group, 0)

    @pl.when(jnp.max(peak) > SLOT)
    def _():
        def cell(a, carry):
            rank = ranks[a]
            pieces = (jnp.max(rank).astype(jnp.int32) + SLOT) // SLOT

            def piece(c, carry):
                base = (c * SLOT).astype(F32)
                pick_i, _, out = edges(lists[a], ranks[a], base, cell_offset(a), own, feats[...], gtab[...], mst[...], wz[...], wr[...])
                s = per_atom(pick_i, out)
                sums_j[a] += s[0:48]
                sums_t[a] += s[48:64]
                return carry

            return lax.fori_loop(1, pieces, piece, carry)

        lax.fori_loop(0, 27, cell, 0)


def wave_kernel(
    sizes, norm, sums_t, sums_j, base9, pack, waves, refrow,
    pots, mine,
    got_t, got_j, cos_h, cos_l, sin_h, sin_l, wrow, part, got_rs, block, got_ar, got_ag, lhs, pot_s,
    st, rt, sj, rj, srs, rrs, sar, rar, sag, rag, sp, rp,
):
    nx, ny, nz = sizes
    plane = [(dx, 0, dz) for dx in range(nx) for dz in range(nz) if (dx, dz) != (0, 0)]
    line = [(0, dy, 0) for dy in range(1, ny)]
    near = [d for _, d in NEAR]
    whom = {tuple((o + s) % s for o, s in zip(d, sizes)) for d in near + plane + line}
    wait = greet(sizes, sorted(whom))
    waves_f = waves[...].astype(F32)
    kvec = [waves_f[d : d + 1] * (2.0 * math.pi / sizes[d]) for d in range(3)]
    ksq = kvec[0] * kvec[0] + kvec[1] * kvec[1] + kvec[2] * kvec[2]
    wrow[0:1] = 2.0 * (8.0 * jnp.exp(ksq * (-1.0 / 64.0)) / (8.0 + ksq) * norm)
    for d in range(3):
        wrow[1 + d : 2 + d] = kvec[d]
    wait()
    first = [send(sums_t.at[i], got_t.at[26 - i], st.at[i], rt.at[i], sizes, d) for i, d in NEAR]
    second = [send(sums_j.at[i], got_j.at[26 - i], sj.at[i], rj.at[i], sizes, d) for i, d in NEAR]
    pos = pack[12:15]
    fields = []
    for d in range(3):
        length = float(sizes[d] * TICKS)
        p = pos[d : d + 1]
        fields.append(((p >> 7).astype(F32), waves_f[d : d + 1] * (128.0 / length)))
        fields.append(((p & 127).astype(F32), waves_f[d : d + 1] * (1.0 / length)))
    zero_i = jnp.zeros((2, 128), F32)
    zero_k = jnp.zeros((2, waves_f.shape[1]), F32)
    pos8 = jnp.concatenate([f[0] for f in fields] + [zero_i], axis=0).astype(BF16)
    wrow[8:16] = jnp.concatenate([f[1] for f in fields] + [zero_k], axis=0)
    blocks = waves_f.shape[1] // 128

    def phase(bi, carry):
        at = pl.ds(pl.multiple_of(bi * 128, 128), 128)
        turn = dot(pos8, wrow[8:16, at].astype(BF16), TN)
        quarter = jnp.floor(turn * 4.0 + 0.5)
        x = (turn - quarter * 0.25) * (2.0 * math.pi)
        qi = quarter.astype(jnp.int32)
        xx = x * x
        s = x * (1.0 + xx * (-1.0 / 6 + xx * (1.0 / 120 + xx * (-1.0 / 5040 + xx * (1.0 / 362880)))))
        c = 1.0 + xx * (-0.5 + xx * (1.0 / 24 + xx * (-1.0 / 720 + xx * (1.0 / 40320))))
        odd = (qi & 1) == 1
        cv = jnp.where(odd, s, c)
        sv = jnp.where(odd, c, s)
        cv = jnp.where(((qi + 1) & 2) == 2, -cv, cv)
        sv = jnp.where((qi & 2) == 2, -sv, sv)
        hi, lo = split(cv)
        cos_h[:, at] = hi
        cos_l[:, at] = lo
        hi, lo = split(sv)
        sin_h[:, at] = hi
        sin_l[:, at] = lo
        return carry

    lax.fori_loop(0, blocks, phase, 0)
    live = jnp.where(iota((1, 128), 1) < pack[15:16], 1.0, 0.0)
    for c in first:
        c.wait()
    total = base9[...] + sums_t[13]
    for i, _ in NEAR:
        total = total + got_t[i]
    q = total[0:8] * live
    qhi, qlo = split(q)
    q16 = jnp.concatenate([qhi, qlo], axis=0)
    for at_row, high, low in ((0, cos_h, cos_l), (8, sin_h, sin_l)):
        s = dot(q16, high[...])
        s = s[0:8] + s[8:16] + dot(q16, low[...])[0:8]
        for bi in range(blocks):
            part[bi, at_row : at_row + 8] = s[:, 128 * bi : 128 * bi + 128]
    ix, iz = lax.axis_index("gx"), lax.axis_index("gz")
    me = ix * nz + iz
    rs = []
    for n, d in enumerate(plane):
        to = lax.rem(ix + d[0], nx) * nz + lax.rem(iz + d[2], nz)
        rs.append(send(part.at[to], got_rs.at[n], srs.at[n], rrs.at[n], sizes, d))
    acc = part[me]
    for n, c in enumerate(rs):
        c.wait()
        acc = acc + got_rs[n]
    block[0] = acc
    ar = [send(block.at[0], got_ar.at[n], sar.at[n], rar.at[n], sizes, d) for n, d in enumerate(line)]
    for n, c in enumerate(ar):
        c.wait()
        acc = acc + got_ar[n]
    got_ag[me] = acc
    ag = [send(got_ag.at[me], got_ag.at[me], sag.at[n], rag.at[n], sizes, d) for n, d in enumerate(plane)]
    for c in ag:
        c.wait()
    width = blocks * 128
    for bi in range(blocks):
        at = slice(128 * bi, 128 * bi + 128)
        weight = wrow[0:1, at]
        pre = got_ag[bi, 0:8] * weight
        pim = got_ag[bi, 8:16] * weight
        kx, ky, kz = wrow[1:2, at], wrow[2:3, at], wrow[3:4, at]
        lc = jnp.concatenate([pre, kx * pim, ky * pim, kz * pim], axis=0)
        ls = jnp.concatenate([pim, -kx * pre, -ky * pre, -kz * pre], axis=0)
        hi, lo = split(lc)
        lhs[0:32, at] = hi
        lhs[32:64, at] = lo
        hi, lo = split(ls)
        lhs[64:96, at] = hi
        lhs[96:128, at] = lo
    w = dot(lhs[0:64], cos_h[...], NT)
    v = dot(lhs[64:128], sin_h[...], NT)
    w = w[0:32] + w[32:64] + dot(lhs[0:32], cos_l[...], NT)
    w = w + v[0:32] + v[32:64] + dot(lhs[64:96], sin_l[...], NT)
    pot = w[0:8]
    flag = jnp.where(iota((8, 128), 0) == 0, live, 0.0)
    pot16 = jnp.concatenate([pot * live, flag], axis=0)
    pot_s[0] = pot16
    third = [send(pot_s.at[0], pots.at[26 - i], sp.at[i], rp.at[i], sizes, d) for i, d in NEAR]
    pots[13] = pot16
    for c in second:
        c.wait()
    js = sums_j[13]
    for i, _ in NEAR:
        js = js + got_j[i]
    rows = []
    for d in range(3):
        wave = jnp.sum(q * w[8 * d + 8 : 8 * d + 16], axis=0, keepdims=True)
        rows.append(wave - jnp.sum(pot16 * js[16 * d : 16 * d + 16], axis=0, keepdims=True))
    site = live * (total[8:9] + refrow[0:1] + 0.5 * jnp.sum(q * pot, axis=0, keepdims=True))
    mine[...] = jnp.concatenate(rows + [site, live, live, live, live], axis=0)
    for c in third:
        c.wait()


def pull_back(pick_i, pick_j, out, pot16):
    hi, lo = split(pot16)
    none = jnp.zeros((16, 128), BF16)
    rep = jnp.concatenate([hi, hi, hi, none, lo, lo, lo, none], axis=0)
    prod = out * dot(pick_i, rep, NT)
    hi, lo = split(prod)
    return dot(hi, pick_j, TN) + dot(lo, pick_j, TN)


def force_kernel(picks_i, picks_j, outs, pots, mine, most, lists, ranks, pack, feats, gtab, mst, wz, wr, site, forces, total):
    def group(gi, acc):
        for u in range(GROUP):
            a = gi * GROUP + u
            acc = acc + pull_back(picks_i[a], picks_j[a], outs[a], pots[a])
        return acc

    total[...] = lax.fori_loop(0, 27 // GROUP, group, jnp.zeros((128, 128), F32))

    @pl.when(jnp.max(most[...]) > SLOT)
    def _():
        own = pack[12:15]

        def cell(a, carry):
            pieces = (jnp.max(ranks[a]).astype(jnp.int32) + SLOT) // SLOT

            def piece(c, carry):
                base = (c * SLOT).astype(F32)
                pick_i, pick_j, out = edges(lists[a], ranks[a], base, cell_offset(a), own, feats[...], gtab[...], mst[...], wz[...], wr[...])
                total[...] += pull_back(pick_i, pick_j, out, pots[a])
                return carry

            return lax.fori_loop(1, pieces, piece, carry)

        lax.fori_loop(0, 27, cell, 0)

    t = total[0:64] + total[64:128]
    live = mine[4:5]
    for d in range(3):
        g = mine[d : d + 1] + jnp.sum(t[16 * d : 16 * d + 16], axis=0, keepdims=True)
        forces[d : d + 1] = -g * live
    site[...] = mine[3:4]


def vmem(n):
    return [pl.BlockSpec(memory_space=pltpu.VMEM)] * n


def shape(dims, kind):
    return jax.ShapeDtypeStruct(dims, kind)


def per_device(
    sizes, features, positions, species, counts, neighbors, waves, radial_in, radial_out,
    species_gain, mix_weight, readout, charge_weight, ref_energy,
):
    nx, ny, nz = sizes
    slots = positions.shape[-1]
    wave_count = waves.shape[1]
    norm = (wave_count * nx * ny * nz * slots) ** -0.5
    feats = features.reshape(slots, -1)
    count_row = jnp.broadcast_to(counts.reshape(1, 1), (1, slots))
    pack = jnp.concatenate([neighbors.reshape(12, slots), positions.reshape(3, slots), count_row], axis=0)
    dma = pltpu.SemaphoreType.DMA
    lists, gtab, mst, wz, wr, base9, refrow = pl.pallas_call(
        functools.partial(spread_kernel, sizes),
        out_shape=[
            shape((27, 16, 128), jnp.int32), shape((128, 256), BF16), shape((256, 128), BF16),
            shape((128, 256), BF16), shape((128, 256), BF16), shape((16, 128), F32), shape((8, 128), F32),
        ],
        in_specs=vmem(10),
        out_specs=vmem(7),
        scratch_shapes=[dma((27,)), dma((27,)), dma],
        compiler_params=pltpu.CompilerParams(collective_id=0, has_side_effects=True),
        name="spread",
    )(
        pack, feats[:, :128], species.reshape(1, slots), radial_in, radial_out, species_gain, mix_weight,
        readout.reshape(1, -1), charge_weight, ref_energy.reshape(1, -1),
    )
    sums_t, sums_j, picks_i, picks_j, outs, ranks, most = pl.pallas_call(
        edge_kernel,
        out_shape=[
            shape((27, 16, 128), F32), shape((27, 48, 128), F32), shape((27, SLOT, 128), BF16),
            shape((27, SLOT, 128), BF16), shape((27, SLOT, 128), F32), shape((27, 16, 128), F32), shape((8, 128), F32),
        ],
        in_specs=vmem(7),
        out_specs=vmem(7),
        scratch_shapes=[pltpu.VMEM((27 * 16, 128), F32)],
        name="edges",
    )(lists, pack, feats, gtab, mst, wz, wr)
    planes, lines = nx * nz, ny
    blocks = wave_count // 128
    buf = pltpu.VMEM
    pots, mine = pl.pallas_call(
        functools.partial(wave_kernel, sizes, norm),
        out_shape=[shape((27, 16, 128), F32), shape((8, 128), F32)],
        in_specs=vmem(6),
        out_specs=vmem(2),
        scratch_shapes=[
            buf((27, 16, 128), F32), buf((27, 48, 128), F32),
            buf((128, wave_count), BF16), buf((128, wave_count), BF16), buf((128, wave_count), BF16), buf((128, wave_count), BF16),
            buf((16, wave_count), F32), buf((blocks, 16, 128), F32), buf((planes - 1, 16, 128), F32), buf((1, 16, 128), F32),
            buf((lines - 1, 16, 128), F32), buf((planes, 16, 128), F32), buf((128, wave_count), BF16), buf((1, 16, 128), F32),
            dma((27,)), dma((27,)), dma((27,)), dma((27,)),
            dma((planes - 1,)), dma((planes - 1,)), dma((lines - 1,)), dma((lines - 1,)),
            dma((planes - 1,)), dma((planes - 1,)), dma((27,)), dma((27,)),
        ],
        compiler_params=pltpu.CompilerParams(collective_id=1, has_side_effects=True),
        name="waves",
    )(sums_t, sums_j, base9, pack, waves, refrow)
    site, forces = pl.pallas_call(
        force_kernel,
        out_shape=[shape((1, 128), F32), shape((3, 128), F32)],
        in_specs=vmem(14),
        out_specs=vmem(2),
        scratch_shapes=[pltpu.VMEM((128, 128), F32)],
        name="forces",
    )(picks_i, picks_j, outs, pots, mine, most, lists, ranks, pack, feats, gtab, mst, wz, wr)
    return site.reshape(1, 1, 1, slots), forces.reshape(1, 1, 1, 3, slots)


def solution(mesh):
    sizes = tuple(mesh.shape[n] for n in AXES)
    cell = P("gx", "gy", "gz")
    placed = (cell,) * 5 + (P(),) * 8
    return jax.shard_map(
        functools.partial(per_device, sizes),
        mesh=mesh,
        in_specs=placed,
        out_specs=(cell, cell),
        check_vma=False,
    )
```

profile of v0, /device:TPU:1, one launch (start us, length us, event | category | flops | bytes accessed | tf_op | source)
XLA Modules:
  0.0 99.1 jit_solution(7614277445907457441)
XLA Ops:
  1.3 0.1 pad.2.clone
  1.4 0.7 copy.22
  2.0 0.7 copy.21
  2.7 0.7 add_add_fusion.pack
  3.4 1.4 %slice.4.feats = bf16[128,128]{1,0:T(8,128)(2,1)} slice(bf16[128,512]{1,0:T(8,128)(2,1)} %bitcast.16), slice={[0:128], [0:128]} | slice | bytes 65536 | tf_op jit(solution)/shard_map/slice | solution.py:444
  4.8 1.4 %copy.15.cw = f32[128,8]{1,0:T(8,128)} copy(f32[128,8]{0,1:T(8,128)} %param.24) | data formatting | bytes 8192 | tf_op args[11]
  6.2 17.9 %spread.1 = (s32[27,16,128]{2,1,0:T(8,128)}, bf16[128,256]{1,0:T(8,128)(2,1)}, bf16[256,128]{1,0:T(8,128)(2,1)}, bf16[128,256]{1,0:T(8,128)(2,1)}, bf16[128,256]...) custom-call(s32[16,128]{1,0:T(8,128)} %add_add_fusion.pack, bf16[128,128]{1,0:T(8,128)(2,1)} %slice.4.feats, ...), custom_call_target="tpu_custom_call" | custom-call | tf_op jit(solution)/shard_map/spread/pallas_call | solution.py:432
  24.1 26.7 %edges.1 = (f32[27,16,128]{2,1,0:T(8,128)}, f32[27,48,128]{2,1,0:T(8,128)}, bf16[27,128,128]{2,1,0:T(8,128)(2,1)}, bf16[27,128,128]{2,1,0:T(8,128)(2,1)}, f32[27...) custom-call(s32[27,16,128]{2,1,0:T(8,128)} %get-tuple-element.20.lists, s32[16,128]{1,0:T(8,128)} %add_add_fusion.pack, ...), custom_call_target="tpu_custom_call" | custom-call | tf_op jit(solution)/shard_map/edges/pallas_call | solution.py:447
  50.8 41.7 %waves.2 = (f32[27,16,128]{2,1,0:T(8,128)}, f32[8,128]{1,0:T(8,128)}) custom-call(f32[27,16,128]{2,1,0:T(8,128)} %get-tuple-element.28.sums_t, f32[27,48,128]{2,1,0:T(8,128)} %get-tuple-element.29.sums_j, f32[16,128]{1,0:T(8,128)} %get-tuple-element.30.base9, s32[16,128]{1,0:T(8,128)} %add_add_fusion.pack, s32[3,2048]{1,0:T(4,128)} %waves.3, ...), custom_call_target="tpu_custom_call" | custom-call | tf_op jit(solution)/shard_map/waves/pallas_call | solution.py:461
  92.5 5.3 %forces.1 = (f32[1,128]{1,0:T(1,128)}, f32[3,128]{1,0:T(4,128)}) custom-call(bf16[27,128,128]{2,1,0:T(8,128)(2,1)} %get-tuple-element.25.picks_i, bf16[27,128,128]{2,1,0:T(8,128)(2,1)} %get-tuple-element.26.picks_j, f32[27,128,128]{2,1,0:T(8,128)} %get-tuple-element.27.outs, f32[27,16,128]{2,1,0:T(8,128)} %get-tuple-element.32.pots, ...), custom_call_target="tpu_custom_call" | custom-call | tf_op jit(solution)/shard_map/forces/pallas_call | solution.py:478
  97.9 1.2 %copy.16 = f32[1,1,1,3,128]{4,2,3,1,0:T(1,128)} copy(f32[1,1,1,3,128]{4,3,2,1,0:T(4,128)} %bitcast.21) | data formatting | bytes 3072
where the time goes:
time: 99.5 us; the launch traced here: 99.1 us
  Pallas kernels  91.7 us (92%)
  local copies, waits for them, and re-layouts  5.47 us (5%)
  between operations  1.3 us (1%)
    pallas_call x1, Pallas kernels, per_device(): pl.pallas_call(functools.partial(wave_kernel, sizes, norm), out_shape=[sh...  41.7 us
    pallas_call x1, Pallas kernels, per_device(): pl.pallas_call(edge_kernel, out_shape=[shape((27, 16, 128), F32), shape((...  26.7 us
    pallas_call x1, Pallas kernels, per_device(): pl.pallas_call(functools.partial(spread_kernel, sizes), out_shape=[shape(...  17.9 us
    pallas_call x1, Pallas kernels, per_device(): pl.pallas_call(force_kernel, out_shape=[shape((1, 128), F32), shape((3, 1...  5.34 us
    unnamed x4, local copies, waits for them, and re-layouts  4.02 us

commit v1 on v0

v1 whole, which is shorter than its diff:
```python
import functools
import math

import jax
import jax.numpy as jnp
from jax import lax
from jax.experimental import pallas as pl
from jax.experimental.pallas import tpu as pltpu
from jax.sharding import PartitionSpec as P

TICKS = 1024
AXES = ("gx", "gy", "gz")
MESH = pl.DeviceIdType.MESH
HIGH = lax.Precision.HIGHEST
OFFS = [(a - 1, b - 1, c - 1) for a in range(3) for b in range(3) for c in range(3)]
F32 = jnp.float32
BF16 = jnp.bfloat16
SLOT = 96
GROUP = 9
LOG2E = math.log2(math.e)
FAR = -1.0e6


def iota(shape, dim):
    return lax.broadcasted_iota(jnp.int32, shape, dim)


def dot(a, b, contract=((1,), (0,)), precision=None):
    return lax.dot_general(a, b, (contract, ((), ())), precision=precision, preferred_element_type=F32)


NT = ((1,), (1,))
TN = ((0,), (0,))


def split(x):
    hi = x.astype(BF16)
    return hi, (x - hi.astype(F32)).astype(BF16)


def at_offset(sizes, d):
    return tuple(lax.rem(lax.axis_index(n) + (s + o), s) if o else lax.axis_index(n) for n, s, o in zip(AXES, sizes, d))


def greet(sizes, offsets):
    barrier = pltpu.get_barrier_semaphore()
    for d in offsets:
        pl.semaphore_signal(barrier, inc=1, device_id=at_offset(sizes, d), device_id_type=MESH)
    return lambda: pl.semaphore_wait(barrier, len(offsets))


def send(src, dst, ssem, rsem, sizes, d):
    c = pltpu.make_async_remote_copy(
        src_ref=src, dst_ref=dst, send_sem=ssem, recv_sem=rsem, device_id=at_offset(sizes, d), device_id_type=MESH
    )
    c.start()
    return c


NEAR = [(i, d) for i, d in enumerate(OFFS) if d != (0, 0, 0)]


SIDE = 128


def rows_of(pos):
    loc = pos & (TICKS - 1)
    scale = 1.0 / TICKS
    return (loc & ~31).astype(F32) * scale, (loc & 31).astype(F32) * scale


def stack(parts):
    return parts[0] if len(parts) == 1 else jnp.concatenate(parts, axis=0)


def edges(blks, ranks, base, offs, own, feats, gtab, mst, wz, wr):
    slot = iota((SLOT, 128), 0).astype(F32) + base
    accs = []
    for blk, rank in zip(blks, ranks):
        code = ((blk & 127) + 1).astype(F32)
        acc = jnp.zeros((SLOT, 128), F32)
        for k in range(12):
            acc = jnp.where(rank[k : k + 1] == slot, code[k : k + 1], acc)
        accs.append(acc)
    picks_i = [jnp.where(acc > 0.0, 1.0, 0.0).astype(BF16) for acc in accs]
    named = dot(stack(accs).astype(BF16), jnp.ones((128, 128), BF16))
    lane = iota(named.shape, 1)
    pick_j = jnp.where(named == (lane + 1).astype(F32), 1.0, 0.0).astype(BF16)
    jhi, jlo = rows_of(own)
    pieces = []
    for n, (blk, off, pick_i) in enumerate(zip(blks, offs, picks_i)):
        ihi, ilo = rows_of(blk[12:15])
        shift = jnp.concatenate([jnp.full((1, 128), o, F32) for o in off], axis=0)
        fill = jnp.zeros((2, 128), F32)
        left = jnp.concatenate([-ihi - shift, -ilo, fill], axis=0)
        right = jnp.concatenate([jhi, jlo, fill], axis=0)
        w = jnp.concatenate([left, right], axis=1).astype(BF16)
        both = jnp.concatenate([pick_i, pick_j[SLOT * n : SLOT * (n + 1)]], axis=1)
        pieces.append(dot(both, w, NT).astype(BF16))
    to_lanes = iota((8, 384), 1) >> 7
    spread = jnp.where((to_lanes == iota((8, 384), 0)) | (to_lanes + 3 == iota((8, 384), 0)), 1.0, 0.0).astype(BF16)
    disp = dot(stack(pieces), spread)
    dx, dy, dz = disp[:, 0:128], disp[:, 128:256], disp[:, 256:384]
    r2 = dx * dx + dy * dy + dz * dz
    s2 = r2 + 0.25
    inv = lax.rsqrt(s2)
    rs = s2 * inv
    inv1 = 1.0 / (1.0 + r2)
    t = rs - (0.25 + 0.5 * lax.rem(iota((1, 128), 1), 8).astype(F32))
    b = jnp.exp2((t * (-2.0 * LOG2E)) * t) * inv1
    b = jnp.where(lane < 8, b, b * (-4.0 * t - 2.0 * rs * inv1)).astype(BF16)
    zz = dot(b, wz)
    z, zp = zz[:, 0:128], zz[:, 128:256]
    sig = 0.5 * jnp.tanh(0.5 * z) + 0.5
    silu = z * sig
    hid = jnp.where(lane < 64, silu, (sig + silu * (1.0 - sig)) * zp).astype(BF16)
    rr = dot(hid, wr)
    g = dot(pick_j, gtab)
    g = g[:, 0:128] + g[:, 128:256]
    rad = rr[:, 0:128] * g
    radp = rr[:, 128:256] * g
    h = dot(pick_j, feats)
    q = []
    for r in (rad, radp):
        for d in range(2):
            x = [(r * h[:, 128 * e : 128 * (e + 1)]).astype(BF16) for e in (2 * d, 2 * d + 1)]
            t = dot(jnp.concatenate(x, axis=1), mst)
            q += [t[:, 0:128], t[:, 128:256]]
    ux, uy, uz = dx * inv, dy * inv, dz * inv
    along = ux * q[1] + uy * q[2] + uz * q[3]
    w = q[4] + ux * q[5] + uy * q[6] + uz * q[7] - along * inv
    part = (lane >> 4) & 3
    ua = jnp.where(part == 0, ux, jnp.where(part == 1, uy, uz))
    qa = jnp.where(part == 0, q[1], jnp.where(part == 1, q[2], q[3]))
    out = jnp.where(part == 3, q[0] + along, ua * w + qa * inv)
    rows = [slice(SLOT * n, SLOT * (n + 1)) for n in range(len(blks))]
    return [(pick_i, pick_j[r], out[r]) for pick_i, r in zip(picks_i, rows)]


def per_atom(pick_i, out):
    lane = iota((SLOT, 128), 1)
    hi = out.astype(BF16)
    mixed = jnp.where(lane < 64, hi.astype(F32), out - hi.astype(F32)).astype(BF16)
    s = dot(mixed, pick_i, TN)
    return s[0:64] + s[64:128]


def cell_offset(a):
    if isinstance(a, int):
        return tuple(float(o) for o in OFFS[a])
    return ((a // 9 - 1).astype(F32), (lax.rem(a // 3, 3) - 1).astype(F32), (lax.rem(a, 3) - 1).astype(F32))


def tables(feats, species, rin, rout, gain, mix, readout, cw, ref_energy, gtab, mst, wz, wr, base9, refrow):
    neigh = 12
    lane = iota((8, SIDE), 1)
    sel8 = jnp.where(lax.rem(lane, 16) == iota((8, SIDE), 0), 1.0, 0.0)
    sel1 = jnp.where(lax.rem(iota((1, SIDE), 1), 16) == 8, 1.0, 0.0)
    rc = dot(cw[...], sel8, TN, HIGH) + dot(readout[...], sel1, TN, HIGH)
    mb = (dot(mix[...].astype(F32), rc, precision=HIGH) * (neigh ** -0.5)).astype(BF16)
    mst[0:128, 0:128] = mb
    mst[0:128, 128:256] = jnp.zeros_like(mb)
    mst[128:256, 0:128] = jnp.zeros_like(mb)
    mst[128:256, 128:256] = mb
    base9[...] = dot(rc, feats[:, 0:128].astype(F32), ((0,), (1,)), HIGH)[0:16]
    kinds = gain.shape[0]
    onehot = jnp.where(iota((kinds, SIDE), 0) == species[...], 1.0, 0.0)
    ghi, glo = split(dot(onehot, gain[...], TN, HIGH))
    gtab[:, 0:128] = ghi
    gtab[:, 128:256] = glo
    refrow[...] = jnp.broadcast_to(dot(ref_energy[...], onehot, precision=HIGH), refrow.shape)
    r = rin[...]
    h = rin.shape[1]
    dup = jnp.where(lax.rem(iota((h, 128), 1), h) == iota((h, 128), 0), 1.0, 0.0).astype(BF16)
    upper = jnp.where(iota((h, 128), 1) - h == iota((h, 128), 0), 1.0, 0.0).astype(BF16)
    rows_a = jnp.where(iota((128, 8), 0) == iota((128, 8), 1), 1.0, 0.0).astype(BF16)
    rows_b = jnp.where(iota((128, 8), 0) - 8 == iota((128, 8), 1), 1.0, 0.0).astype(BF16)
    wz[:, 0:128] = dot(dot(rows_a, r).astype(BF16), dup).astype(BF16)
    wz[:, 128:256] = dot(dot(rows_b, r).astype(BF16), upper).astype(BF16)
    ro = rout[...]
    none = jnp.zeros_like(ro)
    wr[0:64, 0:128] = ro
    wr[64:128, 0:128] = none
    wr[0:64, 128:256] = none
    wr[64:128, 128:256] = ro


def rank_edges(lists, ranks, mask):
    lane = iota((16, 128), 1)
    row = iota((16, 128), 0)
    for a in range(27):
        blk = lists[a]
        keep = ((blk >> 7) == 26 - a) & (lane < blk[15:16]) & (row < 12)
        mask[16 * a : 16 * a + 16] = jnp.where(keep, 1.0, 0.0)
    m = mask[...].astype(BF16)
    tri = jnp.where(iota((128, 128), 0) <= iota((128, 128), 1), 1.0, 0.0).astype(BF16)
    both = dot(m, jnp.concatenate([tri, jnp.ones((128, 128), BF16)], axis=1))
    lower = jnp.where(iota((16, 16), 0) > iota((16, 16), 1), 1.0, 0.0).astype(BF16)
    totals = jnp.concatenate([both[16 * a : 16 * a + 16, 128:256] for a in range(27)], axis=1).astype(BF16)
    start = dot(lower, totals)
    peak = start[12:13, 0:128]
    for a in range(27):
        s = start[:, 128 * a : 128 * a + 128]
        peak = jnp.maximum(peak, s[12:13])
        r = both[16 * a : 16 * a + 16, 0:128] + s - 1.0
        ranks[a] = jnp.where(mask[16 * a : 16 * a + 16] > 0.0, r, FAR)
    return peak


def wave_tables(sizes, norm, waves, pos, wrow):
    waves_f = waves[...].astype(F32)
    kvec = [waves_f[d : d + 1] * (2.0 * math.pi / sizes[d]) for d in range(3)]
    ksq = kvec[0] * kvec[0] + kvec[1] * kvec[1] + kvec[2] * kvec[2]
    wrow[0:1] = 2.0 * (8.0 * jnp.exp(ksq * (-1.0 / 64.0)) / (8.0 + ksq) * norm)
    fields = []
    for d in range(3):
        wrow[1 + d : 2 + d] = kvec[d]
        length = float(sizes[d] * TICKS)
        p = pos[d : d + 1]
        fields.append(((p >> 7).astype(F32), waves_f[d : d + 1] * (128.0 / length)))
        fields.append(((p & 127).astype(F32), waves_f[d : d + 1] * (1.0 / length)))
    zero_i = jnp.zeros((2, 128), F32)
    zero_k = jnp.zeros((2, waves_f.shape[1]), F32)
    wrow[8:16] = jnp.concatenate([f[1] for f in fields] + [zero_k], axis=0)
    return jnp.concatenate([f[0] for f in fields] + [zero_i], axis=0).astype(BF16)


def phases(pos8, wrow, cos_h, cos_l, sin_h, sin_l):
    def phase(bi, carry):
        at = pl.ds(pl.multiple_of(bi * 128, 128), 128)
        turn = dot(pos8, wrow[8:16, at].astype(BF16), TN)
        quarter = jnp.floor(turn * 4.0 + 0.5)
        x = (turn - quarter * 0.25) * (2.0 * math.pi)
        qi = quarter.astype(jnp.int32)
        xx = x * x
        s = x * (1.0 + xx * (-1.0 / 6 + xx * (1.0 / 120 + xx * (-1.0 / 5040 + xx * (1.0 / 362880)))))
        c = 1.0 + xx * (-0.5 + xx * (1.0 / 24 + xx * (-1.0 / 720 + xx * (1.0 / 40320))))
        odd = (qi & 1) == 1
        cv = jnp.where(odd, s, c)
        sv = jnp.where(odd, c, s)
        cv = jnp.where(((qi + 1) & 2) == 2, -cv, cv)
        sv = jnp.where((qi & 2) == 2, -sv, sv)
        hi, lo = split(cv)
        cos_h[:, at] = hi
        cos_l[:, at] = lo
        hi, lo = split(sv)
        sin_h[:, at] = hi
        sin_l[:, at] = lo
        return carry

    lax.fori_loop(0, wrow.shape[1] // 128, phase, 0)


def peers(sizes):
    nx, ny, nz = sizes
    plane = [(dx, 0, dz) for dx in range(nx) for dz in range(nz) if (dx, dz) != (0, 0)]
    line = [(0, dy, 0) for dy in range(1, ny)]
    near = [d for _, d in NEAR]
    whom = {tuple((o + s) % s for o, s in zip(d, sizes)) for d in near + plane + line}
    return plane, line, sorted(whom)


def reciprocal(sizes, poison, sums_t, sums_j, base9, pack, refrow, pots, wrow, trig, bufs, sems):
    nx, ny, nz = sizes
    plane, line, _ = peers(sizes)
    cos_h, cos_l, sin_h, sin_l = trig
    got_t, got_j, part, got_rs, block, got_ar, got_ag, lhs, pot_s = bufs
    st, rt, sj, rj, srs, rrs, sar, rar, sag, rag, sp, rp = sems
    blocks = wrow.shape[1] // 128
    first = [send(sums_t.at[i], got_t.at[26 - i], st.at[i], rt.at[i], sizes, d) for i, d in NEAR]
    live = jnp.where(iota((1, 128), 1) < pack[15:16], 1.0, 0.0)
    total = base9[...] + sums_t[13].astype(F32)
    for c in first:
        c.wait()
    for i, _ in NEAR:
        total = total + got_t[i].astype(F32)
    q = total[0:8] * live
    qhi, qlo = split(q)
    q16 = jnp.concatenate([qhi, qlo], axis=0)
    for at_row, high, low in ((0, cos_h, cos_l), (8, sin_h, sin_l)):
        s = dot(q16, high[...])
        s = s[0:8] + s[8:16] + dot(q16, low[...])[0:8]
        for bi in range(blocks):
            part[bi, at_row : at_row + 8] = s[:, 128 * bi : 128 * bi + 128] + poison
    ix, iz = lax.axis_index("gx"), lax.axis_index("gz")
    me = ix * nz + iz
    rs = []
    for n, d in enumerate(plane):
        to = lax.rem(ix + d[0], nx) * nz + lax.rem(iz + d[2], nz)
        rs.append(send(part.at[to], got_rs.at[n], srs.at[n], rrs.at[n], sizes, d))
    second = [send(sums_j.at[i], got_j.at[26 - i], sj.at[i], rj.at[i], sizes, d) for i, d in NEAR]
    acc = part[me]
    for n, c in enumerate(rs):
        c.wait()
        acc = acc + got_rs[n]
    block[0] = acc
    ar = [send(block.at[0], got_ar.at[n], sar.at[n], rar.at[n], sizes, d) for n, d in enumerate(line)]
    for n, c in enumerate(ar):
        c.wait()
        acc = acc + got_ar[n]
    got_ag[me] = acc
    ag = [send(got_ag.at[me], got_ag.at[me], sag.at[n], rag.at[n], sizes, d) for n, d in enumerate(plane)]
    js = sums_j[13].astype(F32)
    for c in second:
        c.wait()
    for i, _ in NEAR:
        js = js + got_j[i].astype(F32)
    for c in ag:
        c.wait()
    for bi in range(blocks):
        at = slice(128 * bi, 128 * bi + 128)
        weight = wrow[0:1, at]
        pre = got_ag[bi, 0:8] * weight
        pim = got_ag[bi, 8:16] * weight
        kx, ky, kz = wrow[1:2, at], wrow[2:3, at], wrow[3:4, at]
        lc = jnp.concatenate([pre, kx * pim, ky * pim, kz * pim], axis=0)
        ls = jnp.concatenate([pim, -kx * pre, -ky * pre, -kz * pre], axis=0)
        hi, lo = split(lc)
        lhs[0:32, at] = hi
        lhs[32:64, at] = lo
        hi, lo = split(ls)
        lhs[64:96, at] = hi
        lhs[96:128, at] = lo
    w = dot(lhs[0:64], cos_h[...], NT)
    v = dot(lhs[64:128], sin_h[...], NT)
    w = w[0:32] + w[32:64] + dot(lhs[0:32], cos_l[...], NT)
    w = w + v[0:32] + v[32:64] + dot(lhs[64:96], sin_l[...], NT)
    pot = w[0:8]
    flag = jnp.where(iota((8, 128), 0) == 0, live, 0.0)
    pot16 = jnp.concatenate([pot * live, flag], axis=0)
    pot_s[0] = pot16.astype(BF16)
    third = [send(pot_s.at[0], pots.at[26 - i], sp.at[i], rp.at[i], sizes, d) for i, d in NEAR]
    pots[13] = pot16.astype(BF16)
    rows = []
    for d in range(3):
        wave = jnp.sum(q * w[8 * d + 8 : 8 * d + 16], axis=0, keepdims=True)
        rows.append(wave - jnp.sum(pot16 * js[16 * d : 16 * d + 16], axis=0, keepdims=True))
    site = live * (total[8:9] + refrow[0:1] + 0.5 * jnp.sum(q * pot, axis=0, keepdims=True))
    mine = jnp.concatenate(rows + [site, live, live, live, live], axis=0)
    for c in third:
        c.wait()
    return mine


def pull_back(work, pots):
    prods = []
    for (pick_i, _, out), p in zip(work, pots):
        none = jnp.zeros((16, 128), BF16)
        prods.append(out * dot(pick_i, jnp.concatenate([p, p, p, none, p, p, p, none], axis=0), NT))
    prod = stack(prods)
    hi = prod.astype(BF16)
    mixed = jnp.where(iota(prod.shape, 1) < 64, hi.astype(F32), prod - hi.astype(F32)).astype(BF16)
    return dot(mixed, stack([pick_j for _, pick_j, _ in work]), TN)


def give(mine, t, site, forces):
    t = t[0:64] + t[64:128]
    for d in range(3):
        g = mine[d : d + 1] + jnp.sum(t[16 * d : 16 * d + 16], axis=0, keepdims=True)
        forces[d] = -g * mine[4:5]
    site[...] = mine[3:4]


def gather_pack(neighbors, positions, counts, pack, sem):
    copies = [pltpu.make_async_copy(neighbors.at[k], pack.at[pl.ds(k, 1)], sem.at[k]) for k in range(12)]
    copies += [pltpu.make_async_copy(positions.at[d], pack.at[pl.ds(12 + d, 1)], sem.at[12 + d]) for d in range(3)]
    for c in copies:
        c.start()
    pack[15:16] = jnp.full((1, 128), counts[0, 0], jnp.int32)
    return copies


def hand_out(sizes, pack, lists, ssem, rsem):
    copies = [send(pack, lists.at[26 - i], ssem.at[i], rsem.at[i], sizes, d) for i, d in NEAR]
    lists[13] = pack[...]
    return copies


def whole_kernel(
    sizes, norm, neighbors, positions, counts, feats, species, waves, rin, rout, gain, mix, readout, cw, ref_energy,
    site, forces,
    pack, lists, gtab, mst, wz, wr, base9, refrow, ranks, mask, picks_i, picks_j, outs, sums_t, sums_j, pots, wrow,
    cos_h, cos_l, sin_h, sin_l, got_t, got_j, part, got_rs, block, got_ar, got_ag, lhs, pot_s,
    psem, ls, lr, *sems,
):
    wait = greet(sizes, peers(sizes)[2])
    packed = gather_pack(neighbors, positions, counts, pack, psem)
    tables(feats, species, rin, rout, gain, mix, readout, cw, ref_energy, gtab, mst, wz, wr, base9, refrow)
    for c in packed:
        c.wait()
    wait()
    out = hand_out(sizes, pack, lists, ls, lr)
    own = pack[12:15]
    trig = (cos_h, cos_l, sin_h, sin_l)
    phases(wave_tables(sizes, norm, waves, own, wrow), wrow, *trig)
    for c in out:
        c.wait()
    peak = rank_edges(lists, ranks, mask)

    def group(gi, carry):
        cells = [gi * GROUP + u for u in range(GROUP)]
        done = edges(
            [lists[a] for a in cells], [ranks[a] for a in cells], 0.0, [cell_offset(a) for a in cells],
            own, feats[...], gtab[...], mst[...], wz[...], wr[...],
        )
        for a, (pick_i, pick_j, e) in zip(cells, done):
            picks_i[a] = pick_i
            picks_j[a] = pick_j
            outs[a] = e
            s = per_atom(pick_i, e).astype(BF16)
            sums_j[a] = s[0:48]
            sums_t[a] = s[48:64]
        return carry

    lax.fori_loop(0, 27 // GROUP, group, 0)
    poison = jnp.where(peak > float(SLOT), jnp.nan, 0.0)
    bufs = (got_t, got_j, part, got_rs, block, got_ar, got_ag, lhs, pot_s)
    mine = reciprocal(sizes, poison, sums_t, sums_j, base9, pack, refrow, pots, wrow, trig, bufs, sems)

    def back(gi, acc):
        cells = [gi * GROUP + u for u in range(GROUP)]
        return acc + pull_back([(picks_i[a], picks_j[a], outs[a]) for a in cells], [pots[a] for a in cells])

    give(mine, lax.fori_loop(0, 27 // GROUP, back, jnp.zeros((128, 128), F32)), site, forces)


def spread_kernel(
    sizes, neighbors, positions, counts, feats, species, rin, rout, gain, mix, readout, cw, ref_energy,
    lists, pack_out, gtab, mst, wz, wr, base9, refrow, pack, psem, ssem, rsem,
):
    wait = greet(sizes, [d for _, d in NEAR])
    packed = gather_pack(neighbors, positions, counts, pack, psem)
    tables(feats, species, rin, rout, gain, mix, readout, cw, ref_energy, gtab, mst, wz, wr, base9, refrow)
    for c in packed:
        c.wait()
    wait()
    out = hand_out(sizes, pack, lists, ssem, rsem)
    pack_out[...] = pack[...]
    for c in out:
        c.wait()


def each_piece(ranks, run):
    def cell(a, carry):
        pieces = (jnp.max(ranks[a]).astype(jnp.int32) + SLOT) // SLOT
        return lax.fori_loop(0, pieces, lambda c, carry: run(a, (c * SLOT).astype(F32), carry), carry)

    lax.fori_loop(0, 27, cell, 0)


def edge_kernel(lists, pack, feats, gtab, mst, wz, wr, sums_t, sums_j, mask, ranks, total_t, total_j):
    rank_edges(lists, ranks, mask)
    own = pack[12:15]
    total_t[...] = jnp.zeros_like(total_t)
    total_j[...] = jnp.zeros_like(total_j)

    def piece(a, base, carry):
        pick_i, _, out = edges([lists[a]], [ranks[a]], base, [cell_offset(a)], own, feats[...], gtab[...], mst[...], wz[...], wr[...])[0]
        s = per_atom(pick_i, out)
        total_j[a] += s[0:48]
        total_t[a] += s[48:64]
        return carry

    each_piece(ranks, piece)
    sums_t[...] = total_t[...].astype(BF16)
    sums_j[...] = total_j[...].astype(BF16)


def wave_kernel(
    sizes, norm, sums_t, sums_j, base9, pack, waves, refrow, pots, mine,
    wrow, cos_h, cos_l, sin_h, sin_l, got_t, got_j, part, got_rs, block, got_ar, got_ag, lhs, pot_s, *sems,
):
    wait = greet(sizes, peers(sizes)[2])
    trig = (cos_h, cos_l, sin_h, sin_l)
    phases(wave_tables(sizes, norm, waves, pack[12:15], wrow), wrow, *trig)
    wait()
    bufs = (got_t, got_j, part, got_rs, block, got_ar, got_ag, lhs, pot_s)
    mine[...] = reciprocal(sizes, 0.0, sums_t, sums_j, base9, pack, refrow, pots, wrow, trig, bufs, sems)


def force_kernel(pots, mine, lists, pack, feats, gtab, mst, wz, wr, site, forces, mask, ranks, total):
    rank_edges(lists, ranks, mask)
    own = pack[12:15]
    total[...] = jnp.zeros_like(total)

    def piece(a, base, carry):
        work = edges([lists[a]], [ranks[a]], base, [cell_offset(a)], own, feats[...], gtab[...], mst[...], wz[...], wr[...])
        total[...] += pull_back(work, [pots[a]])
        return carry

    each_piece(ranks, piece)
    give(mine[...], total[...], site, forces)


VMEM = pl.BlockSpec(memory_space=pltpu.VMEM)
SMEM = pl.BlockSpec(memory_space=pltpu.SMEM)
HBM = pl.BlockSpec(memory_space=pl.ANY)


def shape(dims, kind):
    return jax.ShapeDtypeStruct(dims, kind)


def wave_buffers(sizes, waves):
    nx, ny, nz = sizes
    planes, blocks = nx * nz, waves // 128
    buf = pltpu.VMEM
    dma = pltpu.SemaphoreType.DMA
    trig = [buf((128, waves), BF16)] * 4
    rest = [
        buf((27, 16, 128), BF16), buf((27, 48, 128), BF16), buf((blocks, 16, 128), F32), buf((planes - 1, 16, 128), F32),
        buf((1, 16, 128), F32), buf((ny - 1, 16, 128), F32), buf((planes, 16, 128), F32), buf((128, waves), BF16),
        buf((1, 16, 128), BF16),
    ]
    counts = (27, 27, 27, 27, planes - 1, planes - 1, ny - 1, ny - 1, planes - 1, planes - 1, 27, 27)
    return [buf((16, waves), F32)] + trig + rest, [dma((n,)) for n in counts]


TABLES = [
    ((128, 256), BF16), ((256, 256), BF16), ((128, 256), BF16), ((128, 256), BF16), ((16, 128), F32), ((8, 128), F32),
]
RANKS = [((27, 16, 128), F32), ((27 * 16, 128), F32)]
RESULT = [((1, 128), F32), ((3, 1, 128), F32)]


def general(sizes, norm, neighbors, positions, counts, feats, species, waves, *params):
    dma = pltpu.SemaphoreType.DMA
    lists, pack, gtab, mst, wz, wr, base9, refrow = pl.pallas_call(
        functools.partial(spread_kernel, sizes),
        out_shape=[shape((27, 16, 128), jnp.int32), shape((16, 128), jnp.int32)] + [shape(*t) for t in TABLES],
        in_specs=[HBM, HBM, SMEM] + [VMEM] * 9,
        out_specs=[VMEM] * 8,
        scratch_shapes=[pltpu.VMEM((16, 128), jnp.int32), dma((15,)), dma((27,)), dma((27,))],
        compiler_params=pltpu.CompilerParams(collective_id=1, has_side_effects=True),
        name="spread",
    )(neighbors, positions, counts, feats, species, *params)
    ranking = [pltpu.VMEM(*RANKS[1]), pltpu.VMEM(*RANKS[0])]
    sums_t, sums_j = pl.pallas_call(
        edge_kernel,
        out_shape=[shape((27, 16, 128), BF16), shape((27, 48, 128), BF16)],
        in_specs=[VMEM] * 7,
        out_specs=[VMEM] * 2,
        scratch_shapes=ranking + [pltpu.VMEM((27, 16, 128), F32), pltpu.VMEM((27, 48, 128), F32)],
        name="edges",
    )(lists, pack, feats, gtab, mst, wz, wr)
    bufs, sems = wave_buffers(sizes, waves.shape[1])
    pots, mine = pl.pallas_call(
        functools.partial(wave_kernel, sizes, norm),
        out_shape=[shape((27, 16, 128), BF16), shape((8, 128), F32)],
        in_specs=[VMEM] * 6,
        out_specs=[VMEM] * 2,
        scratch_shapes=bufs + sems,
        compiler_params=pltpu.CompilerParams(collective_id=2, has_side_effects=True),
        name="waves",
    )(sums_t, sums_j, base9, pack, waves, refrow)
    return pl.pallas_call(
        force_kernel,
        out_shape=[shape(*r) for r in RESULT],
        in_specs=[VMEM] * 9,
        out_specs=[VMEM] * 2,
        scratch_shapes=ranking + [pltpu.VMEM((128, 128), F32)],
        name="forces",
    )(pots, mine, lists, pack, feats, gtab, mst, wz, wr)


def direct(sizes, norm, neighbors, positions, counts, feats, species, waves, *params):
    dma = pltpu.SemaphoreType.DMA
    buf = pltpu.VMEM
    bufs, sems = wave_buffers(sizes, waves.shape[1])
    scratch = [buf((16, 128), jnp.int32), buf((27, 16, 128), jnp.int32)] + [buf(*t) for t in TABLES + RANKS]
    scratch += [buf((27, SLOT, 128), BF16), buf((27, SLOT, 128), BF16), buf((27, SLOT, 128), F32)]
    scratch += [buf((27, 16, 128), BF16), buf((27, 48, 128), BF16), buf((27, 16, 128), BF16)]
    return pl.pallas_call(
        functools.partial(whole_kernel, sizes, norm),
        out_shape=[shape(*r) for r in RESULT],
        in_specs=[HBM, HBM, SMEM] + [VMEM] * 10,
        out_specs=[VMEM] * 2,
        scratch_shapes=scratch + bufs + [dma((15,)), dma((27,)), dma((27,))] + sems,
        compiler_params=pltpu.CompilerParams(collective_id=0, has_side_effects=True),
        name="whole",
    )(neighbors, positions, counts, feats, species, waves, *params)


def per_device(
    sizes, features, positions, species, counts, neighbors, waves, radial_in, radial_out,
    species_gain, mix_weight, readout, charge_weight, ref_energy,
):
    nx, ny, nz = sizes
    slots = positions.shape[-1]
    norm = (waves.shape[1] * nx * ny * nz * slots) ** -0.5
    args = (
        neighbors.reshape(12, 1, slots), positions.reshape(3, 1, slots), counts.reshape(1, 1),
        features.reshape(slots, -1), species.reshape(1, slots), waves, radial_in, radial_out, species_gain,
        mix_weight, readout.reshape(1, -1), charge_weight.T, ref_energy.reshape(1, -1),
    )
    site, forces = direct(sizes, norm, *args)
    crowded = jnp.isnan(site[0, 0])
    site, forces = lax.cond(
        crowded, lambda s, f, *a: tuple(general(sizes, norm, *a)), lambda s, f, *a: (s, f), site, forces, *args
    )
    return site.reshape(1, 1, 1, slots), forces.reshape(1, 1, 1, 3, slots)


def solution(mesh):
    sizes = tuple(mesh.shape[n] for n in AXES)
    cell = P("gx", "gy", "gz")
    placed = (cell,) * 5 + (P(),) * 8
    return jax.shard_map(
        functools.partial(per_device, sizes),
        mesh=mesh,
        in_specs=placed,
        out_specs=(cell, cell),
        check_vma=False,
    )
```

time: 99.5 us -> 63.3 us (0.64)
  Pallas kernels: 91.7 us -> 59.2 us
  local copies, waits for them, and re-layouts: 5.47 us -> 2.34 us
    pallas_call x4 -> x1, Pallas kernels: 91.7 us -> 59.2 us  [direct(): pl.pallas_call(functools.partial(whole_kernel, sizes, norm), out_shape=[s...]
    unnamed x4 -> x26, local copies, waits for them, and re-layouts: 4.02 us -> 2.34 us
    slice x1 -> x0, local copies, waits for them, and re-layouts: 1.37 us -> none  [per_device(): feats[:, :128]]
where the time goes in v1:
time: 63.3 us; the launch traced here: 63 us
  Pallas kernels  59.2 us (94%)
  local copies, waits for them, and re-layouts  2.34 us (4%)
  between operations  1.47 us (2%)
    pallas_call x1, Pallas kernels, direct(): pl.pallas_call(functools.partial(whole_kernel, sizes, norm), out_shape=[s...  59.2 us
    unnamed x26, local copies, waits for them, and re-layouts  2.34 us

profile of v1, /device:TPU:1, one launch (start us, length us, event | category | flops | bytes accessed | tf_op | source)
XLA Modules:
  0.0 63.0 jit_solution(11014224131512540671)
XLA Ops:
  0.6 0.0 copy-start.3
  1.3 0.0 copy-start.6
  1.3 0.0 copy-start.9
  1.3 0.0 copy-start
  1.3 0.0 copy-done.3
  1.4 0.6 %copy-done.6 = f32[128,8]{0,1:T(8,128)S(1)} copy-done((f32[128,8]{0,1:T(8,128)S(1)}, f32[128,8]{0,1:T(8,128)}, u32[]{:S(2)}) %copy-start.6) | copy-done | bytes 4120
  2.0 0.0 copy-done.9
  2.0 0.0 copy-start.1
  2.0 0.0 copy-start.2
  2.0 0.0 copy-start.4
  2.0 0.0 copy-start.7
  2.0 0.0 copy-start.10
  2.0 0.0 copy-start.11
  2.0 59.2 %whole.1 = (f32[1,128]{1,0:T(1,128)S(1)}, f32[3,1,128]{2,1,0:T(1,128)S(1)}) custom-call(s32[12,1,128]{2,1,0:T(1,128)} %bitcast.17, s32[3,1,128]{2,1,0:T(1,128)} %bitcast.21, s32[1,1]{1,0:T(1,128)} %bitcast.14.counts, bf16[128,512]{1,0:T(8,128)(2,1)} %bitcast.15, s32[1,128]{1,0:T(1,128)S(1)} %bitcast.23, s32[3,2048]{1,0:T(4,128)} %waves.3, ...), custom_call_target="tpu_custom_call" | custom-call | tf_op jit(solution)/shard_map/whole/pallas_call | solution.py:573
  61.2 0.0 copy-start.5
  61.3 0.0 copy-start.8
  61.3 0.0 copy-done
  61.3 0.0 copy-done.1
  61.3 0.0 copy-done.2
  61.3 0.0 copy-done.4
  61.4 0.0 copy-done.7
  61.4 0.0 copy-done.10
  61.4 0.0 copy-done.11
  61.4 0.6 copy-done.5
  61.9 0.0 copy-done.8
  62.0 0.5 copy.22
  62.5 0.6 copy.23
  (1 shorter events, 0.0 us)
Async XLA Ops:
  0.6 0.7 %copy-start.3 = (bf16[64,128]{1,0:T(8,128)(2,1)S(1)}, bf16[64,128]{1,0:T(8,128)(2,1)}, u32[]{:S(2)}) copy-start(bf16[64,128]{1,0:T(8,128)(2,1)} %rout.1) | copy-start | bytes 49156
  1.3 0.7 %copy-start.6 = (f32[128,8]{0,1:T(8,128)S(1)}, f32[128,8]{0,1:T(8,128)}, u32[]{:S(2)}) copy-start(f32[128,8]{0,1:T(8,128)} %param.26) | copy-start | bytes 12292
  1.3 0.7 %copy-start.9 = (s32[1,1,1,128]{3,2,1,0:T(1,128)S(1)}, s32[1,1,1,128]{3,2,1,0:T(1,128)}, u32[]{:S(2)}) copy-start(s32[1,1,1,128]{3,2,1,0:T(1,128)} %param.17) | copy-start | bytes 1540
  1.3 60.0 %copy-start = (bf16[1,1,1,128,512]{4,3,2,1,0:T(8,128)(2,1)S(1)}, bf16[1,1,1,128,512]{4,3,2,1,0:T(8,128)(2,1)}, u32[]{:S(2)}) copy-start(bf16[1,1,1,128,512]{4,3,2,1,0:T(8,128)(2,1)} %param.15) | copy-start | bytes 393220
  2.0 59.3 %copy-start.1 = (bf16[128,128]{1,0:T(8,128)(2,1)S(1)}, bf16[128,128]{1,0:T(8,128)(2,1)}, u32[]{:S(2)}) copy-start(bf16[128,128]{1,0:T(8,128)(2,1)} %mix.1) | copy-start | bytes 98308
  2.0 59.3 %copy-start.2 = (s32[3,2048]{1,0:T(4,128)S(1)}, s32[3,2048]{1,0:T(4,128)}, u32[]{:S(2)}) copy-start(s32[3,2048]{1,0:T(4,128)} %waves.3) | copy-start | bytes 73732
  2.0 59.3 %copy-start.4 = (f32[10,128]{1,0:T(8,128)S(1)}, f32[10,128]{1,0:T(8,128)}, u32[]{:S(2)}) copy-start(f32[10,128]{1,0:T(8,128)} %gain.1) | copy-start | bytes 15364
  2.0 59.3 %copy-start.7 = (bf16[8,64]{1,0:T(8,128)(2,1)S(1)}, bf16[8,64]{1,0:T(8,128)(2,1)}, u32[]{:S(2)}) copy-start(bf16[8,64]{1,0:T(8,128)(2,1)} %rin.1) | copy-start | bytes 3076
  2.0 59.3 %copy-start.10 = (f32[128]{0:T(128)S(1)}, f32[128]{0:T(128)}, u32[]{:S(2)}) copy-start(f32[128]{0:T(128)} %param.25) | copy-start | bytes 1540
  2.0 59.3 %copy-start.11 = (f32[10]{0:T(128)S(1)}, f32[10]{0:T(128)}, u32[]{:S(2)}) copy-start(f32[10]{0:T(128)} %param.27) | copy-start | bytes 124
  61.2 0.7 %copy-start.5 = (s32[1,1,1,12,128]{4,2,3,1,0:T(1,128)S(1)}, s32[1,1,1,12,128]{4,2,3,1,0:T(1,128)}, u32[]{:S(2)}) copy-start(s32[1,1,1,12,128]{4,2,3,1,0:T(1,128)} %param.19) | copy-start | bytes 18436
  61.3 0.7 %copy-start.8 = (s32[1,1,1,3,128]{4,2,3,1,0:T(1,128)S(1)}, s32[1,1,1,3,128]{4,2,3,1,0:T(1,128)}, u32[]{:S(2)}) copy-start(s32[1,1,1,3,128]{4,2,3,1,0:T(1,128)} %param.16) | copy-start | bytes 4612

commit v2 on v1

--- a/solution.py
+++ b/solution.py
@@ -42,16 +42,22 @@
     return tuple(lax.rem(lax.axis_index(n) + (s + o), s) if o else lax.axis_index(n) for n, s, o in zip(AXES, sizes, d))
 
 
-def greet(sizes, offsets):
+def in_plane(sizes, d):
+    dx, flip, dz = d
+    x, y, z = at_offset(sizes, (dx, 0, dz))
+    return x, y + 1 - 2 * lax.rem(y, 2) if flip else y, z
+
+
+def greet(devices):
     barrier = pltpu.get_barrier_semaphore()
-    for d in offsets:
-        pl.semaphore_signal(barrier, inc=1, device_id=at_offset(sizes, d), device_id_type=MESH)
-    return lambda: pl.semaphore_wait(barrier, len(offsets))
-
-
-def send(src, dst, ssem, rsem, sizes, d):
+    for device in devices:
+        pl.semaphore_signal(barrier, inc=1, device_id=device, device_id_type=MESH)
+    return lambda: pl.semaphore_wait(barrier, len(devices))
+
+
+def send(src, dst, ssem, rsem, device):
     c = pltpu.make_async_remote_copy(
-        src_ref=src, dst_ref=dst, send_sem=ssem, recv_sem=rsem, device_id=at_offset(sizes, d), device_id_type=MESH
+        src_ref=src, dst_ref=dst, send_sem=ssem, recv_sem=rsem, device_id=device, device_id_type=MESH
     )
     c.start()
     return c
@@ -253,11 +259,12 @@
 
 def peers(sizes):
     nx, ny, nz = sizes
-    plane = [(dx, 0, dz) for dx in range(nx) for dz in range(nz) if (dx, dz) != (0, 0)]
-    line = [(0, dy, 0) for dy in range(1, ny)]
+    plane = [(dx, flip, dz) for dx in range(nx) for flip in range(2) for dz in range(nz)][1:]
+    line = [(0, dy, 0) for dy in range(2, ny, 2)]
     near = [d for _, d in NEAR]
-    whom = {tuple((o + s) % s for o, s in zip(d, sizes)) for d in near + plane + line}
-    return plane, line, sorted(whom)
+    known = [((d[0] + nx) % nx, abs(d[1]), (d[2] + nz) % nz) for d in near]
+    whom = [at_offset(sizes, d) for d in near + line] + [in_plane(sizes, d) for d in plane if d not in known]
+    return plane, line, whom
 
 
 def reciprocal(sizes, poison, sums_t, sums_j, base9, pack, refrow, pots, wrow, trig, bufs, sems):
@@ -267,7 +274,7 @@
     got_t, got_j, part, got_rs, block, got_ar, got_ag, lhs, pot_s = bufs
     st, rt, sj, rj, srs, rrs, sar, rar, sag, rag, sp, rp = sems
     blocks = wrow.shape[1] // 128
-    first = [send(sums_t.at[i], got_t.at[26 - i], st.at[i], rt.at[i], sizes, d) for i, d in NEAR]
+    first = [send(sums_t.at[i], got_t.at[26 - i], st.at[i], rt.at[i], at_offset(sizes, d)) for i, d in NEAR]
     live = jnp.where(iota((1, 128), 1) < pack[15:16], 1.0, 0.0)
     total = base9[...] + sums_t[13].astype(F32)
     for c in first:
@@ -277,29 +284,30 @@
     q = total[0:8] * live
     qhi, qlo = split(q)
     q16 = jnp.concatenate([qhi, qlo], axis=0)
-    for at_row, high, low in ((0, cos_h, cos_l), (8, sin_h, sin_l)):
+    for half, high, low in ((0, cos_h, cos_l), (1, sin_h, sin_l)):
         s = dot(q16, high[...])
         s = s[0:8] + s[8:16] + dot(q16, low[...])[0:8]
         for bi in range(blocks):
-            part[bi, at_row : at_row + 8] = s[:, 128 * bi : 128 * bi + 128] + poison
-    ix, iz = lax.axis_index("gx"), lax.axis_index("gz")
-    me = ix * nz + iz
+            part[2 * bi + half] = s[:, 128 * bi : 128 * bi + 128] + poison
+    ix, iy, iz = [lax.axis_index(n) for n in AXES]
+    low_x = lax.rem(iy, 2)
+    me = (ix * 2 + low_x) * nz + iz
     rs = []
     for n, d in enumerate(plane):
-        to = lax.rem(ix + d[0], nx) * nz + lax.rem(iz + d[2], nz)
-        rs.append(send(part.at[to], got_rs.at[n], srs.at[n], rrs.at[n], sizes, d))
-    second = [send(sums_j.at[i], got_j.at[26 - i], sj.at[i], rj.at[i], sizes, d) for i, d in NEAR]
+        to = (lax.rem(ix + d[0], nx) * 2 + (1 - low_x if d[1] else low_x)) * nz + lax.rem(iz + d[2], nz)
+        rs.append(send(part.at[to], got_rs.at[n], srs.at[n], rrs.at[n], in_plane(sizes, d)))
+    second = [send(sums_j.at[i], got_j.at[26 - i], sj.at[i], rj.at[i], at_offset(sizes, d)) for i, d in NEAR]
     acc = part[me]
     for n, c in enumerate(rs):
         c.wait()
         acc = acc + got_rs[n]
     block[0] = acc
-    ar = [send(block.at[0], got_ar.at[n], sar.at[n], rar.at[n], sizes, d) for n, d in enumerate(line)]
+    ar = [send(block.at[0], got_ar.at[n], sar.at[n], rar.at[n], at_offset(sizes, d)) for n, d in enumerate(line)]
     for n, c in enumerate(ar):
         c.wait()
         acc = acc + got_ar[n]
     got_ag[me] = acc
-    ag = [send(got_ag.at[me], got_ag.at[me], sag.at[n], rag.at[n], sizes, d) for n, d in enumerate(plane)]
+    ag = [send(got_ag.at[me], got_ag.at[me], sag.at[n], rag.at[n], in_plane(sizes, d)) for n, d in enumerate(plane)]
     js = sums_j[13].astype(F32)
     for c in second:
         c.wait()
@@ -310,8 +318,8 @@
     for bi in range(blocks):
         at = slice(128 * bi, 128 * bi + 128)
         weight = wrow[0:1, at]
-        pre = got_ag[bi, 0:8] * weight
-        pim = got_ag[bi, 8:16] * weight
+        pre = got_ag[2 * bi] * weight
+        pim = got_ag[2 * bi + 1] * weight
         kx, ky, kz = wrow[1:2, at], wrow[2:3, at], wrow[3:4, at]
         lc = jnp.concatenate([pre, kx * pim, ky * pim, kz * pim], axis=0)
         ls = jnp.concatenate([pim, -kx * pre, -ky * pre, -kz * pre], axis=0)
@@ -329,7 +337,7 @@
     flag = jnp.where(iota((8, 128), 0) == 0, live, 0.0)
     pot16 = jnp.concatenate([pot * live, flag], axis=0)
     pot_s[0] = pot16.astype(BF16)
-    third = [send(pot_s.at[0], pots.at[26 - i], sp.at[i], rp.at[i], sizes, d) for i, d in NEAR]
+    third = [send(pot_s.at[0], pots.at[26 - i], sp.at[i], rp.at[i], at_offset(sizes, d)) for i, d in NEAR]
     pots[13] = pot16.astype(BF16)
     rows = []
     for d in range(3):
@@ -371,20 +379,32 @@
 
 
 def hand_out(sizes, pack, lists, ssem, rsem):
-    copies = [send(pack, lists.at[26 - i], ssem.at[i], rsem.at[i], sizes, d) for i, d in NEAR]
+    copies = [send(pack, lists.at[26 - i], ssem.at[i], rsem.at[i], at_offset(sizes, d)) for i, d in NEAR]
     lists[13] = pack[...]
     return copies
 
 
 def whole_kernel(
-    sizes, norm, neighbors, positions, counts, feats, species, waves, rin, rout, gain, mix, readout, cw, ref_energy,
-    site, forces,
-    pack, lists, gtab, mst, wz, wr, base9, refrow, ranks, mask, picks_i, picks_j, outs, sums_t, sums_j, pots, wrow,
+    sizes, norm, neighbors, positions, counts, *rest,
+):
+    far, (site, forces), near = rest[:10], rest[10:12], rest[12:22]
+    whole_steps(sizes, norm, neighbors, positions, counts, far, near, site, forces, *rest[22:])
+
+
+def whole_steps(
+    sizes, norm, neighbors, positions, counts, far, near, site, forces,
+    osem, pack, lists, gtab, mst, wz, wr, base9, refrow, ranks, mask, picks_i, picks_j, outs, sums_t, sums_j, pots, wrow,
     cos_h, cos_l, sin_h, sin_l, got_t, got_j, part, got_rs, block, got_ar, got_ag, lhs, pot_s,
     psem, ls, lr, *sems,
 ):
-    wait = greet(sizes, peers(sizes)[2])
+    wait = greet(peers(sizes)[2])
     packed = gather_pack(neighbors, positions, counts, pack, psem)
+    brought = [pltpu.make_async_copy(f, n, osem.at[i]) for i, (f, n) in enumerate(zip(far, near))]
+    for c in brought:
+        c.start()
+    for c in brought:
+        c.wait()
+    feats, species, waves, rin, rout, gain, mix, readout, cw, ref_energy = near
     tables(feats, species, rin, rout, gain, mix, readout, cw, ref_energy, gtab, mst, wz, wr, base9, refrow)
     for c in packed:
         c.wait()
@@ -428,7 +448,7 @@
     sizes, neighbors, positions, counts, feats, species, rin, rout, gain, mix, readout, cw, ref_energy,
     lists, pack_out, gtab, mst, wz, wr, base9, refrow, pack, psem, ssem, rsem,
 ):
-    wait = greet(sizes, [d for _, d in NEAR])
+    wait = greet([at_offset(sizes, d) for _, d in NEAR])
     packed = gather_pack(neighbors, positions, counts, pack, psem)
     tables(feats, species, rin, rout, gain, mix, readout, cw, ref_energy, gtab, mst, wz, wr, base9, refrow)
     for c in packed:
@@ -470,7 +490,7 @@
     sizes, norm, sums_t, sums_j, base9, pack, waves, refrow, pots, mine,
     wrow, cos_h, cos_l, sin_h, sin_l, got_t, got_j, part, got_rs, block, got_ar, got_ag, lhs, pot_s, *sems,
 ):
-    wait = greet(sizes, peers(sizes)[2])
+    wait = greet(peers(sizes)[2])
     trig = (cos_h, cos_l, sin_h, sin_l)
     phases(wave_tables(sizes, norm, waves, pack[12:15], wrow), wrow, *trig)
     wait()
@@ -494,7 +514,7 @@
 
 VMEM = pl.BlockSpec(memory_space=pltpu.VMEM)
 SMEM = pl.BlockSpec(memory_space=pltpu.SMEM)
-HBM = pl.BlockSpec(memory_space=pl.ANY)
+HBM = pl.BlockSpec(memory_space=pltpu.HBM)
 
 
 def shape(dims, kind):
@@ -503,16 +523,17 @@
 
 def wave_buffers(sizes, waves):
     nx, ny, nz = sizes
-    planes, blocks = nx * nz, waves // 128
+    planes, lines = 2 * nx * nz, ny // 2
+    assert planes == 2 * waves // 128
     buf = pltpu.VMEM
     dma = pltpu.SemaphoreType.DMA
     trig = [buf((128, waves), BF16)] * 4
     rest = [
-        buf((27, 16, 128), BF16), buf((27, 48, 128), BF16), buf((blocks, 16, 128), F32), buf((planes - 1, 16, 128), F32),
-        buf((1, 16, 128), F32), buf((ny - 1, 16, 128), F32), buf((planes, 16, 128), F32), buf((128, waves), BF16),
+        buf((27, 16, 128), BF16), buf((27, 48, 128), BF16), buf((planes, 8, 128), F32), buf((planes - 1, 8, 128), F32),
+        buf((1, 8, 128), F32), buf((lines - 1, 8, 128), F32), buf((planes, 8, 128), F32), buf((128, waves), BF16),
         buf((1, 16, 128), BF16),
     ]
-    counts = (27, 27, 27, 27, planes - 1, planes - 1, ny - 1, ny - 1, planes - 1, planes - 1, 27, 27)
+    counts = (27, 27, 27, 27, planes - 1, planes - 1, lines - 1, lines - 1, planes - 1, planes - 1, 27, 27)
     return [buf((16, waves), F32)] + trig + rest, [dma((n,)) for n in counts]
 
 
@@ -567,13 +588,15 @@
     dma = pltpu.SemaphoreType.DMA
     buf = pltpu.VMEM
     bufs, sems = wave_buffers(sizes, waves.shape[1])
-    scratch = [buf((16, 128), jnp.int32), buf((27, 16, 128), jnp.int32)] + [buf(*t) for t in TABLES + RANKS]
+    brought = (feats, species, waves) + params
+    scratch = [buf(b.shape, b.dtype) for b in brought] + [dma((len(brought),))]
+    scratch += [buf((16, 128), jnp.int32), buf((27, 16, 128), jnp.int32)] + [buf(*t) for t in TABLES + RANKS]
     scratch += [buf((27, SLOT, 128), BF16), buf((27, SLOT, 128), BF16), buf((27, SLOT, 128), F32)]
     scratch += [buf((27, 16, 128), BF16), buf((27, 48, 128), BF16), buf((27, 16, 128), BF16)]
     return pl.pallas_call(
         functools.partial(whole_kernel, sizes, norm),
         out_shape=[shape(*r) for r in RESULT],
-        in_specs=[HBM, HBM, SMEM] + [VMEM] * 10,
+        in_specs=[HBM, HBM, SMEM] + [HBM] * 10,
         out_specs=[VMEM] * 2,
         scratch_shapes=scratch + bufs + [dma((15,)), dma((27,)), dma((27,))] + sems,
         compiler_params=pltpu.CompilerParams(collective_id=0, has_side_effects=True),

time: 63.3 us -> 61 us (0.964)
  Pallas kernels: 59.2 us -> 57 us
    pallas_call x1, Pallas kernels: 59.2 us -> 57 us  [direct(): pl.pallas_call(functools.partial(whole_kernel, sizes, norm), out_shape=[s...]
where the time goes in v2:
time: 61 us; the launch traced here: 60.8 us
  Pallas kernels  57 us (93%)
  local copies, waits for them, and re-layouts  2.34 us (4%)
  between operations  1.47 us (2%)
    pallas_call x1, Pallas kernels, direct(): pl.pallas_call(functools.partial(whole_kernel, sizes, norm), out_shape=[s...  57 us
    unnamed x26, local copies, waits for them, and re-layouts  2.34 us

profile of v2, /device:TPU:1, one launch (start us, length us, event | category | flops | bytes accessed | tf_op | source)
XLA Modules:
  0.0 60.8 jit_solution(2577943050981472778)
XLA Ops:
  0.6 0.0 copy-start.3
  1.3 0.0 copy-start.6
  1.3 0.0 copy-start.9
  1.3 0.0 copy-start
  1.3 0.0 copy-done.3
  1.4 0.6 %copy-done.6 = f32[128,8]{0,1:T(8,128)S(1)} copy-done((f32[128,8]{0,1:T(8,128)S(1)}, f32[128,8]{0,1:T(8,128)}, u32[]{:S(2)}) %copy-start.6) | copy-done | bytes 4120
  2.0 0.0 copy-done.9
  2.0 0.0 copy-start.1
  2.0 0.0 copy-start.2
  2.0 0.0 copy-start.4
  2.0 0.0 copy-start.7
  2.0 0.0 copy-start.10
  2.0 0.0 copy-start.11
  2.0 57.0 %whole.1 = (f32[1,128]{1,0:T(1,128)S(1)}, f32[3,1,128]{2,1,0:T(1,128)S(1)}) custom-call(s32[12,1,128]{2,1,0:T(1,128)} %bitcast.17, s32[3,1,128]{2,1,0:T(1,128)} %bitcast.21, s32[1,1]{1,0:T(1,128)} %bitcast.14.counts, bf16[128,512]{1,0:T(8,128)(2,1)} %bitcast.15, s32[1,128]{1,0:T(1,128)S(1)} %bitcast.23, s32[3,2048]{1,0:T(4,128)} %rest_2_.1, ...), custom_call_target="tpu_custom_call" | custom-call | tf_op jit(solution)/shard_map/whole/pallas_call | solution.py:596
  59.0 0.0 copy-start.5
  59.0 0.0 copy-start.8
  59.1 0.0 copy-done
  59.1 0.0 copy-done.1
  59.1 0.0 copy-done.2
  59.1 0.0 copy-done.4
  59.1 0.0 copy-done.7
  59.1 0.0 copy-done.10
  59.1 0.0 copy-done.11
  59.1 0.6 copy-done.5
  59.7 0.0 copy-done.8
  59.7 0.5 copy.22
  60.2 0.6 copy.23
  (1 shorter events, 0.0 us)
Async XLA Ops:
  0.6 0.7 %copy-start.3 = (bf16[64,128]{1,0:T(8,128)(2,1)S(1)}, bf16[64,128]{1,0:T(8,128)(2,1)}, u32[]{:S(2)}) copy-start(bf16[64,128]{1,0:T(8,128)(2,1)} %rest_4_.1) | copy-start | bytes 49156
  1.3 0.7 %copy-start.6 = (f32[128,8]{0,1:T(8,128)S(1)}, f32[128,8]{0,1:T(8,128)}, u32[]{:S(2)}) copy-start(f32[128,8]{0,1:T(8,128)} %param.26) | copy-start | bytes 12292
  1.3 0.7 %copy-start.9 = (s32[1,1,1,128]{3,2,1,0:T(1,128)S(1)}, s32[1,1,1,128]{3,2,1,0:T(1,128)}, u32[]{:S(2)}) copy-start(s32[1,1,1,128]{3,2,1,0:T(1,128)} %param.17) | copy-start | bytes 1540
  1.3 57.7 %copy-start = (bf16[1,1,1,128,512]{4,3,2,1,0:T(8,128)(2,1)S(1)}, bf16[1,1,1,128,512]{4,3,2,1,0:T(8,128)(2,1)}, u32[]{:S(2)}) copy-start(bf16[1,1,1,128,512]{4,3,2,1,0:T(8,128)(2,1)} %param.15) | copy-start | bytes 393220
  2.0 57.1 %copy-start.1 = (bf16[128,128]{1,0:T(8,128)(2,1)S(1)}, bf16[128,128]{1,0:T(8,128)(2,1)}, u32[]{:S(2)}) copy-start(bf16[128,128]{1,0:T(8,128)(2,1)} %rest_6_.1) | copy-start | bytes 98308
  2.0 57.1 %copy-start.2 = (s32[3,2048]{1,0:T(4,128)S(1)}, s32[3,2048]{1,0:T(4,128)}, u32[]{:S(2)}) copy-start(s32[3,2048]{1,0:T(4,128)} %rest_2_.1) | copy-start | bytes 73732
  2.0 57.1 %copy-start.4 = (f32[10,128]{1,0:T(8,128)S(1)}, f32[10,128]{1,0:T(8,128)}, u32[]{:S(2)}) copy-start(f32[10,128]{1,0:T(8,128)} %rest_5_.1) | copy-start | bytes 15364
  2.0 57.1 %copy-start.7 = (bf16[8,64]{1,0:T(8,128)(2,1)S(1)}, bf16[8,64]{1,0:T(8,128)(2,1)}, u32[]{:S(2)}) copy-start(bf16[8,64]{1,0:T(8,128)(2,1)} %rest_3_.1) | copy-start | bytes 3076
  2.0 57.1 %copy-start.10 = (f32[128]{0:T(128)S(1)}, f32[128]{0:T(128)}, u32[]{:S(2)}) copy-start(f32[128]{0:T(128)} %param.25) | copy-start | bytes 1540
  2.0 57.1 %copy-start.11 = (f32[10]{0:T(128)S(1)}, f32[10]{0:T(128)}, u32[]{:S(2)}) copy-start(f32[10]{0:T(128)} %param.27) | copy-start | bytes 124
  59.0 0.7 %copy-start.5 = (s32[1,1,1,12,128]{4,2,3,1,0:T(1,128)S(1)}, s32[1,1,1,12,128]{4,2,3,1,0:T(1,128)}, u32[]{:S(2)}) copy-start(s32[1,1,1,12,128]{4,2,3,1,0:T(1,128)} %param.19) | copy-start | bytes 18436
  59.0 0.7 %copy-start.8 = (s32[1,1,1,3,128]{4,2,3,1,0:T(1,128)S(1)}, s32[1,1,1,3,128]{4,2,3,1,0:T(1,128)}, u32[]{:S(2)}) copy-start(s32[1,1,1,3,128]{4,2,3,1,0:T(1,128)} %param.16) | copy-start | bytes 4612

commit v3 on v2

--- a/solution.py
+++ b/solution.py
@@ -19,6 +19,7 @@
 GROUP = 9
 LOG2E = math.log2(math.e)
 FAR = -1.0e6
+LIST = jnp.int16
 
 
 def iota(shape, dim):
@@ -75,11 +76,15 @@
     return (loc & ~31).astype(F32) * scale, (loc & 31).astype(F32) * scale
 
 
+def wide(x):
+    return x.astype(jnp.int32)
+
+
 def stack(parts):
     return parts[0] if len(parts) == 1 else jnp.concatenate(parts, axis=0)
 
 
-def edges(blks, ranks, base, offs, own, feats, gtab, mst, wz, wr):
+def find(blks, ranks, base):
     slot = iota((SLOT, 128), 0).astype(F32) + base
     accs = []
     for blk, rank in zip(blks, ranks):
@@ -91,7 +96,10 @@
     picks_i = [jnp.where(acc > 0.0, 1.0, 0.0).astype(BF16) for acc in accs]
     named = dot(stack(accs).astype(BF16), jnp.ones((128, 128), BF16))
     lane = iota(named.shape, 1)
-    pick_j = jnp.where(named == (lane + 1).astype(F32), 1.0, 0.0).astype(BF16)
+    return picks_i, jnp.where(named == (lane + 1).astype(F32), 1.0, 0.0).astype(BF16)
+
+
+def distance(blks, offs, own, picks_i, pick_j):
     jhi, jlo = rows_of(own)
     pieces = []
     for n, (blk, off, pick_i) in enumerate(zip(blks, offs, picks_i)):
@@ -105,7 +113,10 @@
         pieces.append(dot(both, w, NT).astype(BF16))
     to_lanes = iota((8, 384), 1) >> 7
     spread = jnp.where((to_lanes == iota((8, 384), 0)) | (to_lanes + 3 == iota((8, 384), 0)), 1.0, 0.0).astype(BF16)
-    disp = dot(stack(pieces), spread)
+    return dot(stack(pieces), spread)
+
+
+def basis(disp):
     dx, dy, dz = disp[:, 0:128], disp[:, 128:256], disp[:, 256:384]
     r2 = dx * dx + dy * dy + dz * dz
     s2 = r2 + 0.25
@@ -114,15 +125,38 @@
     inv1 = 1.0 / (1.0 + r2)
     t = rs - (0.25 + 0.5 * lax.rem(iota((1, 128), 1), 8).astype(F32))
     b = jnp.exp2((t * (-2.0 * LOG2E)) * t) * inv1
+    return (dx * inv, dy * inv, dz * inv), inv, rs, inv1, t, b
+
+
+def sigmoid(z):
+    return 0.5 * jnp.tanh(0.5 * z) + 0.5
+
+
+def gains(pick_j, gtab):
+    g = dot(pick_j, gtab)
+    return g[:, 0:128] + g[:, 128:256]
+
+
+def forward(disp, pick_j, feats, gtab, mst, wz, wr):
+    (ux, uy, uz), _, _, _, _, b = basis(disp)
+    z = dot(b.astype(BF16), wz[:, 0:128])
+    rad = dot((z * sigmoid(z)).astype(BF16), wr[:, 0:128]) * gains(pick_j, gtab)
+    h = dot(pick_j, feats)
+    x = h[:, 0:128] + ux * h[:, 128:256] + uy * h[:, 256:384] + uz * h[:, 384:512]
+    return dot((rad * x).astype(BF16), mst[0:128, 0:128])
+
+
+def slopes(disp, pick_j, feats, gtab, mst, wz, wr):
+    lane = iota((disp.shape[0], 128), 1)
+    (ux, uy, uz), inv, rs, inv1, t, b = basis(disp)
     b = jnp.where(lane < 8, b, b * (-4.0 * t - 2.0 * rs * inv1)).astype(BF16)
     zz = dot(b, wz)
     z, zp = zz[:, 0:128], zz[:, 128:256]
-    sig = 0.5 * jnp.tanh(0.5 * z) + 0.5
+    sig = sigmoid(z)
     silu = z * sig
     hid = jnp.where(lane < 64, silu, (sig + silu * (1.0 - sig)) * zp).astype(BF16)
     rr = dot(hid, wr)
-    g = dot(pick_j, gtab)
-    g = g[:, 0:128] + g[:, 128:256]
+    g = gains(pick_j, gtab)
     rad = rr[:, 0:128] * g
     radp = rr[:, 128:256] * g
     h = dot(pick_j, feats)
@@ -132,15 +166,17 @@
             x = [(r * h[:, 128 * e : 128 * (e + 1)]).astype(BF16) for e in (2 * d, 2 * d + 1)]
             t = dot(jnp.concatenate(x, axis=1), mst)
             q += [t[:, 0:128], t[:, 128:256]]
-    ux, uy, uz = dx * inv, dy * inv, dz * inv
     along = ux * q[1] + uy * q[2] + uz * q[3]
     w = q[4] + ux * q[5] + uy * q[6] + uz * q[7] - along * inv
     part = (lane >> 4) & 3
     ua = jnp.where(part == 0, ux, jnp.where(part == 1, uy, uz))
     qa = jnp.where(part == 0, q[1], jnp.where(part == 1, q[2], q[3]))
-    out = jnp.where(part == 3, q[0] + along, ua * w + qa * inv)
-    rows = [slice(SLOT * n, SLOT * (n + 1)) for n in range(len(blks))]
-    return [(pick_i, pick_j[r], out[r]) for pick_i, r in zip(picks_i, rows)]
+    return jnp.where(part == 3, q[0] + along, ua * w + qa * inv)
+
+
+def edges(blk, rank, base, off, own, *tabs):
+    picks_i, pick_j = find([blk], [rank], base)
+    return picks_i[0], pick_j, slopes(distance([blk], [off], own, picks_i, pick_j), pick_j, *tabs)
 
 
 def per_atom(pick_i, out):
@@ -195,7 +231,7 @@
     lane = iota((16, 128), 1)
     row = iota((16, 128), 0)
     for a in range(27):
-        blk = lists[a]
+        blk = wide(lists[a])
         keep = ((blk >> 7) == 26 - a) & (lane < blk[15:16]) & (row < 12)
         mask[16 * a : 16 * a + 16] = jnp.where(keep, 1.0, 0.0)
     m = mask[...].astype(BF16)
@@ -267,7 +303,7 @@
     return plane, line, whom
 
 
-def reciprocal(sizes, poison, sums_t, sums_j, base9, pack, refrow, pots, wrow, trig, bufs, sems):
+def reciprocal(sizes, poison, sums_t, sums_j, base9, pack, refrow, pots, wrow, trig, bufs, sems, meanwhile=lambda n: None):
     nx, ny, nz = sizes
     plane, line, _ = peers(sizes)
     cos_h, cos_l, sin_h, sin_l = trig
@@ -277,6 +313,7 @@
     first = [send(sums_t.at[i], got_t.at[26 - i], st.at[i], rt.at[i], at_offset(sizes, d)) for i, d in NEAR]
     live = jnp.where(iota((1, 128), 1) < pack[15:16], 1.0, 0.0)
     total = base9[...] + sums_t[13].astype(F32)
+    meanwhile(0)
     for c in first:
         c.wait()
     for i, _ in NEAR:
@@ -296,23 +333,20 @@
     for n, d in enumerate(plane):
         to = (lax.rem(ix + d[0], nx) * 2 + (1 - low_x if d[1] else low_x)) * nz + lax.rem(iz + d[2], nz)
         rs.append(send(part.at[to], got_rs.at[n], srs.at[n], rrs.at[n], in_plane(sizes, d)))
-    second = [send(sums_j.at[i], got_j.at[26 - i], sj.at[i], rj.at[i], at_offset(sizes, d)) for i, d in NEAR]
+    meanwhile(1)
     acc = part[me]
     for n, c in enumerate(rs):
         c.wait()
         acc = acc + got_rs[n]
     block[0] = acc
     ar = [send(block.at[0], got_ar.at[n], sar.at[n], rar.at[n], at_offset(sizes, d)) for n, d in enumerate(line)]
+    meanwhile(2)
     for n, c in enumerate(ar):
         c.wait()
         acc = acc + got_ar[n]
     got_ag[me] = acc
     ag = [send(got_ag.at[me], got_ag.at[me], sag.at[n], rag.at[n], in_plane(sizes, d)) for n, d in enumerate(plane)]
-    js = sums_j[13].astype(F32)
-    for c in second:
-        c.wait()
-    for i, _ in NEAR:
-        js = js + got_j[i].astype(F32)
+    second = [send(sums_j.at[i], got_j.at[26 - i], sj.at[i], rj.at[i], at_offset(sizes, d)) for i, d in NEAR]
     for c in ag:
         c.wait()
     for bi in range(blocks):
@@ -339,6 +373,11 @@
     pot_s[0] = pot16.astype(BF16)
     third = [send(pot_s.at[0], pots.at[26 - i], sp.at[i], rp.at[i], at_offset(sizes, d)) for i, d in NEAR]
     pots[13] = pot16.astype(BF16)
+    js = sums_j[13].astype(F32)
+    for c in second:
+        c.wait()
+    for i, _ in NEAR:
+        js = js + got_j[i].astype(F32)
     rows = []
     for d in range(3):
         wave = jnp.sum(q * w[8 * d + 8 : 8 * d + 16], axis=0, keepdims=True)
@@ -384,6 +423,12 @@
     return copies
 
 
+def shorten(pack, short):
+    row = iota((16, 128), 0)
+    local = (row >= 12) & (row < 15)
+    short[...] = jnp.where(local, pack[...] & (TICKS - 1), pack[...]).astype(LIST)
+
+
 def whole_kernel(
     sizes, norm, neighbors, positions, counts, *rest,
 ):
@@ -393,7 +438,7 @@
 
 def whole_steps(
     sizes, norm, neighbors, positions, counts, far, near, site, forces,
-    osem, pack, lists, gtab, mst, wz, wr, base9, refrow, ranks, mask, picks_i, picks_j, outs, sums_t, sums_j, pots, wrow,
+    osem, pack, short, lists, gtab, mst, wz, wr, base9, refrow, ranks, mask, picks_i, picks_j, outs, sums_t, sums_j, pots, wrow,
     cos_h, cos_l, sin_h, sin_l, got_t, got_j, part, got_rs, block, got_ar, got_ag, lhs, pot_s,
     psem, ls, lr, *sems,
 ):
@@ -408,8 +453,9 @@
     tables(feats, species, rin, rout, gain, mix, readout, cw, ref_energy, gtab, mst, wz, wr, base9, refrow)
     for c in packed:
         c.wait()
+    shorten(pack, short)
     wait()
-    out = hand_out(sizes, pack, lists, ls, lr)
+    out = hand_out(sizes, short, lists, ls, lr)
     own = pack[12:15]
     trig = (cos_h, cos_l, sin_h, sin_l)
     phases(wave_tables(sizes, norm, waves, own, wrow), wrow, *trig)
@@ -417,25 +463,36 @@
         c.wait()
     peak = rank_edges(lists, ranks, mask)
 
-    def group(gi, carry):
+    tabs = (feats, gtab, mst, wz, wr)
+
+    def first(gi, carry):
         cells = [gi * GROUP + u for u in range(GROUP)]
-        done = edges(
-            [lists[a] for a in cells], [ranks[a] for a in cells], 0.0, [cell_offset(a) for a in cells],
-            own, feats[...], gtab[...], mst[...], wz[...], wr[...],
-        )
-        for a, (pick_i, pick_j, e) in zip(cells, done):
-            picks_i[a] = pick_i
-            picks_j[a] = pick_j
-            outs[a] = e
-            s = per_atom(pick_i, e).astype(BF16)
-            sums_j[a] = s[0:48]
-            sums_t[a] = s[48:64]
+        blks = [wide(lists[a]) for a in cells]
+        found, pick_j = find(blks, [ranks[a] for a in cells], 0.0)
+        disp = distance(blks, [cell_offset(a) for a in cells], own, found, pick_j)
+        out = forward(disp, pick_j, *[t[...] for t in tabs])
+        for n, a in enumerate(cells):
+            rows = slice(SLOT * n, SLOT * n + SLOT)
+            picks_i[a] = found[n]
+            picks_j[a] = pick_j[rows]
+            sums_t[a] = per_atom(found[n], out[rows])[0:16].astype(BF16)
         return carry
 
-    lax.fori_loop(0, 27 // GROUP, group, 0)
+    def later(gi):
+        cells = [gi * GROUP + u for u in range(GROUP)]
+        found = [picks_i[a] for a in cells]
+        pick_j = stack([picks_j[a] for a in cells])
+        disp = distance([wide(lists[a]) for a in cells], [cell_offset(a) for a in cells], own, found, pick_j)
+        out = slopes(disp, pick_j, *[t[...] for t in tabs])
+        for n, a in enumerate(cells):
+            rows = slice(SLOT * n, SLOT * n + SLOT)
+            outs[a] = out[rows]
+            sums_j[a] = per_atom(found[n], out[rows])[0:48].astype(BF16)
+
+    lax.fori_loop(0, 27 // GROUP, first, 0)
     poison = jnp.where(peak > float(SLOT), jnp.nan, 0.0)
     bufs = (got_t, got_j, part, got_rs, block, got_ar, got_ag, lhs, pot_s)
-    mine = reciprocal(sizes, poison, sums_t, sums_j, base9, pack, refrow, pots, wrow, trig, bufs, sems)
+    mine = reciprocal(sizes, poison, sums_t, sums_j, base9, pack, refrow, pots, wrow, trig, bufs, sems, later)
 
     def back(gi, acc):
         cells = [gi * GROUP + u for u in range(GROUP)]
@@ -446,15 +503,16 @@
 
 def spread_kernel(
     sizes, neighbors, positions, counts, feats, species, rin, rout, gain, mix, readout, cw, ref_energy,
-    lists, pack_out, gtab, mst, wz, wr, base9, refrow, pack, psem, ssem, rsem,
+    lists, pack_out, gtab, mst, wz, wr, base9, refrow, pack, short, psem, ssem, rsem,
 ):
     wait = greet([at_offset(sizes, d) for _, d in NEAR])
     packed = gather_pack(neighbors, positions, counts, pack, psem)
     tables(feats, species, rin, rout, gain, mix, readout, cw, ref_energy, gtab, mst, wz, wr, base9, refrow)
     for c in packed:
         c.wait()
+    shorten(pack, short)
     wait()
-    out = hand_out(sizes, pack, lists, ssem, rsem)
+    out = hand_out(sizes, short, lists, ssem, rsem)
     pack_out[...] = pack[...]
     for c in out:
         c.wait()
@@ -475,7 +533,7 @@
     total_j[...] = jnp.zeros_like(total_j)
 
     def piece(a, base, carry):
-        pick_i, _, out = edges([lists[a]], [ranks[a]], base, [cell_offset(a)], own, feats[...], gtab[...], mst[...], wz[...], wr[...])[0]
+        pick_i, _, out = edges(wide(lists[a]), ranks[a], base, cell_offset(a), own, feats[...], gtab[...], mst[...], wz[...], wr[...])
         s = per_atom(pick_i, out)
         total_j[a] += s[0:48]
         total_t[a] += s[48:64]
@@ -504,8 +562,8 @@
     total[...] = jnp.zeros_like(total)
 
     def piece(a, base, carry):
-        work = edges([lists[a]], [ranks[a]], base, [cell_offset(a)], own, feats[...], gtab[...], mst[...], wz[...], wr[...])
-        total[...] += pull_back(work, [pots[a]])
+        work = edges(wide(lists[a]), ranks[a], base, cell_offset(a), own, feats[...], gtab[...], mst[...], wz[...], wr[...])
+        total[...] += pull_back([work], [pots[a]])
         return carry
 
     each_piece(ranks, piece)
@@ -548,10 +606,10 @@
     dma = pltpu.SemaphoreType.DMA
     lists, pack, gtab, mst, wz, wr, base9, refrow = pl.pallas_call(
         functools.partial(spread_kernel, sizes),
-        out_shape=[shape((27, 16, 128), jnp.int32), shape((16, 128), jnp.int32)] + [shape(*t) for t in TABLES],
+        out_shape=[shape((27, 16, 128), LIST), shape((16, 128), jnp.int32)] + [shape(*t) for t in TABLES],
         in_specs=[HBM, HBM, SMEM] + [VMEM] * 9,
         out_specs=[VMEM] * 8,
-        scratch_shapes=[pltpu.VMEM((16, 128), jnp.int32), dma((15,)), dma((27,)), dma((27,))],
+        scratch_shapes=[pltpu.VMEM((16, 128), jnp.int32), pltpu.VMEM((16, 128), LIST), dma((15,)), dma((27,)), dma((27,))],
         compiler_params=pltpu.CompilerParams(collective_id=1, has_side_effects=True),
         name="spread",
     )(neighbors, positions, counts, feats, species, *params)
@@ -590,7 +648,7 @@
     bufs, sems = wave_buffers(sizes, waves.shape[1])
     brought = (feats, species, waves) + params
     scratch = [buf(b.shape, b.dtype) for b in brought] + [dma((len(brought),))]
-    scratch += [buf((16, 128), jnp.int32), buf((27, 16, 128), jnp.int32)] + [buf(*t) for t in TABLES + RANKS]
+    scratch += [buf((16, 128), jnp.int32), buf((16, 128), LIST), buf((27, 16, 128), LIST)] + [buf(*t) for t in TABLES + RANKS]
     scratch += [buf((27, SLOT, 128), BF16), buf((27, SLOT, 128), BF16), buf((27, SLOT, 128), F32)]
     scratch += [buf((27, 16, 128), BF16), buf((27, 48, 128), BF16), buf((27, 16, 128), BF16)]
     return pl.pallas_call(

time: 61 us -> 59.4 us (0.974)
  Pallas kernels: 57 us -> 55.3 us
    pallas_call x1, Pallas kernels: 57 us -> 55.3 us  [direct(): pl.pallas_call(functools.partial(whole_kernel, sizes, norm), out_shape=[s...]
where the time goes in v3:
time: 59.4 us; the launch traced here: 59.1 us
  Pallas kernels  55.3 us (93%)
  local copies, waits for them, and re-layouts  2.34 us (4%)
  between operations  1.47 us (2%)
    pallas_call x1, Pallas kernels, direct(): pl.pallas_call(functools.partial(whole_kernel, sizes, norm), out_shape=[s...  55.3 us
    unnamed x26, local copies, waits for them, and re-layouts  2.34 us

profile of v3, /device:TPU:1, one launch (start us, length us, event | category | flops | bytes accessed | tf_op | source)
XLA Modules:
  0.0 59.1 jit_solution(6448967586919839483)
XLA Ops:
  0.6 0.0 copy-start.3
  1.3 0.0 copy-start.6
  1.3 0.0 copy-start.9
  1.3 0.0 copy-start
  1.3 0.0 copy-done.3
  1.4 0.6 %copy-done.6 = f32[128,8]{0,1:T(8,128)S(1)} copy-done((f32[128,8]{0,1:T(8,128)S(1)}, f32[128,8]{0,1:T(8,128)}, u32[]{:S(2)}) %copy-start.6) | copy-done | bytes 4120
  2.0 0.0 copy-done.9
  2.0 0.0 copy-start.1
  2.0 0.0 copy-start.2
  2.0 0.0 copy-start.4
  2.0 0.0 copy-start.7
  2.0 0.0 copy-start.10
  2.0 0.0 copy-start.11
  2.0 55.3 %whole.1 = (f32[1,128]{1,0:T(1,128)S(1)}, f32[3,1,128]{2,1,0:T(1,128)S(1)}) custom-call(s32[12,1,128]{2,1,0:T(1,128)} %bitcast.17, s32[3,1,128]{2,1,0:T(1,128)} %bitcast.21, s32[1,1]{1,0:T(1,128)} %bitcast.14.counts, bf16[128,512]{1,0:T(8,128)(2,1)} %bitcast.15, s32[1,128]{1,0:T(1,128)S(1)} %bitcast.23, s32[3,2048]{1,0:T(4,128)} %rest_2_.1, ...), custom_call_target="tpu_custom_call" | custom-call | tf_op jit(solution)/shard_map/whole/pallas_call | solution.py:654
  57.3 0.0 copy-start.5
  57.3 0.0 copy-start.8
  57.4 0.0 copy-done
  57.4 0.0 copy-done.1
  57.4 0.0 copy-done.2
  57.4 0.0 copy-done.4
  57.4 0.0 copy-done.7
  57.4 0.0 copy-done.10
  57.5 0.0 copy-done.11
  57.5 0.6 copy-done.5
  58.0 0.0 copy-done.8
  58.0 0.5 copy.22
  58.5 0.6 copy.23
  (1 shorter events, 0.0 us)
Async XLA Ops:
  0.6 0.7 %copy-start.3 = (bf16[64,128]{1,0:T(8,128)(2,1)S(1)}, bf16[64,128]{1,0:T(8,128)(2,1)}, u32[]{:S(2)}) copy-start(bf16[64,128]{1,0:T(8,128)(2,1)} %rest_4_.1) | copy-start | bytes 49156
  1.3 0.7 %copy-start.6 = (f32[128,8]{0,1:T(8,128)S(1)}, f32[128,8]{0,1:T(8,128)}, u32[]{:S(2)}) copy-start(f32[128,8]{0,1:T(8,128)} %param.26) | copy-start | bytes 12292
  1.3 0.7 %copy-start.9 = (s32[1,1,1,128]{3,2,1,0:T(1,128)S(1)}, s32[1,1,1,128]{3,2,1,0:T(1,128)}, u32[]{:S(2)}) copy-start(s32[1,1,1,128]{3,2,1,0:T(1,128)} %param.17) | copy-start | bytes 1540
  1.3 56.1 %copy-start = (bf16[1,1,1,128,512]{4,3,2,1,0:T(8,128)(2,1)S(1)}, bf16[1,1,1,128,512]{4,3,2,1,0:T(8,128)(2,1)}, u32[]{:S(2)}) copy-start(bf16[1,1,1,128,512]{4,3,2,1,0:T(8,128)(2,1)} %param.15) | copy-start | bytes 393220
  2.0 55.4 %copy-start.1 = (bf16[128,128]{1,0:T(8,128)(2,1)S(1)}, bf16[128,128]{1,0:T(8,128)(2,1)}, u32[]{:S(2)}) copy-start(bf16[128,128]{1,0:T(8,128)(2,1)} %rest_6_.1) | copy-start | bytes 98308
  2.0 55.4 %copy-start.2 = (s32[3,2048]{1,0:T(4,128)S(1)}, s32[3,2048]{1,0:T(4,128)}, u32[]{:S(2)}) copy-start(s32[3,2048]{1,0:T(4,128)} %rest_2_.1) | copy-start | bytes 73732
  2.0 55.4 %copy-start.4 = (f32[10,128]{1,0:T(8,128)S(1)}, f32[10,128]{1,0:T(8,128)}, u32[]{:S(2)}) copy-start(f32[10,128]{1,0:T(8,128)} %rest_5_.1) | copy-start | bytes 15364
  2.0 55.4 %copy-start.7 = (bf16[8,64]{1,0:T(8,128)(2,1)S(1)}, bf16[8,64]{1,0:T(8,128)(2,1)}, u32[]{:S(2)}) copy-start(bf16[8,64]{1,0:T(8,128)(2,1)} %rest_3_.1) | copy-start | bytes 3076
  2.0 55.4 %copy-start.10 = (f32[128]{0:T(128)S(1)}, f32[128]{0:T(128)}, u32[]{:S(2)}) copy-start(f32[128]{0:T(128)} %param.25) | copy-start | bytes 1540
  2.0 55.4 %copy-start.11 = (f32[10]{0:T(128)S(1)}, f32[10]{0:T(128)}, u32[]{:S(2)}) copy-start(f32[10]{0:T(128)} %param.27) | copy-start | bytes 124
  57.3 0.7 %copy-start.5 = (s32[1,1,1,12,128]{4,2,3,1,0:T(1,128)S(1)}, s32[1,1,1,12,128]{4,2,3,1,0:T(1,128)}, u32[]{:S(2)}) copy-start(s32[1,1,1,12,128]{4,2,3,1,0:T(1,128)} %param.19) | copy-start | bytes 18436
  57.3 0.7 %copy-start.8 = (s32[1,1,1,3,128]{4,2,3,1,0:T(1,128)S(1)}, s32[1,1,1,3,128]{4,2,3,1,0:T(1,128)}, u32[]{:S(2)}) copy-start(s32[1,1,1,3,128]{4,2,3,1,0:T(1,128)} %param.16) | copy-start | bytes 4612

commit v4 on v3

--- a/solution.py
+++ b/solution.py
@@ -64,7 +64,9 @@
     return c
 
 
-NEAR = [(i, d) for i, d in enumerate(OFFS) if d != (0, 0, 0)]
+LEVEL = [i for i, d in enumerate(OFFS) if d[0] == 0]
+APART = [i for i, d in enumerate(OFFS) if d[0] != 0]
+NEAR = [(i, OFFS[i]) for i in LEVEL + APART if i != 13]
 
 
 SIDE = 128
@@ -227,25 +229,26 @@
     wr[64:128, 128:256] = ro
 
 
-def rank_edges(lists, ranks, mask):
+def rank_edges(lists, ranks, mask, cells):
     lane = iota((16, 128), 1)
     row = iota((16, 128), 0)
-    for a in range(27):
+    many = len(cells)
+    for n, a in enumerate(cells):
         blk = wide(lists[a])
         keep = ((blk >> 7) == 26 - a) & (lane < blk[15:16]) & (row < 12)
-        mask[16 * a : 16 * a + 16] = jnp.where(keep, 1.0, 0.0)
-    m = mask[...].astype(BF16)
+        mask[16 * n : 16 * n + 16] = jnp.where(keep, 1.0, 0.0)
+    m = mask[0 : 16 * many].astype(BF16)
     tri = jnp.where(iota((128, 128), 0) <= iota((128, 128), 1), 1.0, 0.0).astype(BF16)
     both = dot(m, jnp.concatenate([tri, jnp.ones((128, 128), BF16)], axis=1))
     lower = jnp.where(iota((16, 16), 0) > iota((16, 16), 1), 1.0, 0.0).astype(BF16)
-    totals = jnp.concatenate([both[16 * a : 16 * a + 16, 128:256] for a in range(27)], axis=1).astype(BF16)
+    totals = jnp.concatenate([both[16 * n : 16 * n + 16, 128:256] for n in range(many)], axis=1).astype(BF16)
     start = dot(lower, totals)
     peak = start[12:13, 0:128]
-    for a in range(27):
-        s = start[:, 128 * a : 128 * a + 128]
+    for n, a in enumerate(cells):
+        s = start[:, 128 * n : 128 * n + 128]
         peak = jnp.maximum(peak, s[12:13])
-        r = both[16 * a : 16 * a + 16, 0:128] + s - 1.0
-        ranks[a] = jnp.where(mask[16 * a : 16 * a + 16] > 0.0, r, FAR)
+        r = both[16 * n : 16 * n + 16, 0:128] + s - 1.0
+        ranks[a] = jnp.where(mask[16 * n : 16 * n + 16] > 0.0, r, FAR)
     return peak
 
 
@@ -303,14 +306,13 @@
     return plane, line, whom
 
 
-def reciprocal(sizes, poison, sums_t, sums_j, base9, pack, refrow, pots, wrow, trig, bufs, sems, meanwhile=lambda n: None):
+def reciprocal(sizes, poison, first, sums_t, sums_j, base9, pack, refrow, pots, wrow, trig, bufs, sems, meanwhile=lambda n: None):
     nx, ny, nz = sizes
     plane, line, _ = peers(sizes)
     cos_h, cos_l, sin_h, sin_l = trig
     got_t, got_j, part, got_rs, block, got_ar, got_ag, lhs, pot_s = bufs
-    st, rt, sj, rj, srs, rrs, sar, rar, sag, rag, sp, rp = sems
+    _, _, sj, rj, srs, rrs, sar, rar, sag, rag, sp, rp = sems
     blocks = wrow.shape[1] // 128
-    first = [send(sums_t.at[i], got_t.at[26 - i], st.at[i], rt.at[i], at_offset(sizes, d)) for i, d in NEAR]
     live = jnp.where(iota((1, 128), 1) < pack[15:16], 1.0, 0.0)
     total = base9[...] + sums_t[13].astype(F32)
     meanwhile(0)
@@ -384,9 +386,13 @@
         rows.append(wave - jnp.sum(pot16 * js[16 * d : 16 * d + 16], axis=0, keepdims=True))
     site = live * (total[8:9] + refrow[0:1] + 0.5 * jnp.sum(q * pot, axis=0, keepdims=True))
     mine = jnp.concatenate(rows + [site, live, live, live, live], axis=0)
-    for c in third:
-        c.wait()
-    return mine
+    return mine, third
+
+
+def hand_sums(sizes, sums_t, got_t, ssem, rsem, cells):
+    return [
+        send(sums_t.at[i], got_t.at[26 - i], ssem.at[i], rsem.at[i], at_offset(sizes, d)) for i, d in NEAR if i in cells
+    ]
 
 
 def pull_back(work, pots):
@@ -459,14 +465,9 @@
     own = pack[12:15]
     trig = (cos_h, cos_l, sin_h, sin_l)
     phases(wave_tables(sizes, norm, waves, own, wrow), wrow, *trig)
-    for c in out:
-        c.wait()
-    peak = rank_edges(lists, ranks, mask)
-
     tabs = (feats, gtab, mst, wz, wr)
 
-    def first(gi, carry):
-        cells = [gi * GROUP + u for u in range(GROUP)]
+    def first(cells):
         blks = [wide(lists[a]) for a in cells]
         found, pick_j = find(blks, [ranks[a] for a in cells], 0.0)
         disp = distance(blks, [cell_offset(a) for a in cells], own, found, pick_j)
@@ -476,7 +477,6 @@
             picks_i[a] = found[n]
             picks_j[a] = pick_j[rows]
             sums_t[a] = per_atom(found[n], out[rows])[0:16].astype(BF16)
-        return carry
 
     def later(gi):
         cells = [gi * GROUP + u for u in range(GROUP)]
@@ -489,16 +489,25 @@
             outs[a] = out[rows]
             sums_j[a] = per_atom(found[n], out[rows])[0:48].astype(BF16)
 
-    lax.fori_loop(0, 27 // GROUP, first, 0)
+    peak = jnp.zeros((1, 128), F32)
+    sums = []
+    for cells in (LEVEL, APART):
+        here = [n for n, (i, _) in enumerate(NEAR) if i in cells]
+        for n in here:
+            out[n].wait()
+        peak = jnp.maximum(peak, rank_edges(lists, ranks, mask, cells))
+        first(cells)
+        sums += hand_sums(sizes, sums_t, got_t, sems[0], sems[1], cells)
     poison = jnp.where(peak > float(SLOT), jnp.nan, 0.0)
     bufs = (got_t, got_j, part, got_rs, block, got_ar, got_ag, lhs, pot_s)
-    mine = reciprocal(sizes, poison, sums_t, sums_j, base9, pack, refrow, pots, wrow, trig, bufs, sems, later)
-
-    def back(gi, acc):
-        cells = [gi * GROUP + u for u in range(GROUP)]
-        return acc + pull_back([(picks_i[a], picks_j[a], outs[a]) for a in cells], [pots[a] for a in cells])
-
-    give(mine, lax.fori_loop(0, 27 // GROUP, back, jnp.zeros((128, 128), F32)), site, forces)
+    mine, third = reciprocal(sizes, poison, sums, sums_t, sums_j, base9, pack, refrow, pots, wrow, trig, bufs, sems, later)
+    total = jnp.zeros((128, 128), F32)
+    for cells in (LEVEL, APART):
+        for n, (i, _) in enumerate(NEAR):
+            if i in cells:
+                third[n].wait()
+        total = total + pull_back([(picks_i[a], picks_j[a], outs[a]) for a in cells], [pots[a] for a in cells])
+    give(mine, total, site, forces)
 
 
 def spread_kernel(
@@ -527,7 +536,7 @@
 
 
 def edge_kernel(lists, pack, feats, gtab, mst, wz, wr, sums_t, sums_j, mask, ranks, total_t, total_j):
-    rank_edges(lists, ranks, mask)
+    rank_edges(lists, ranks, mask, range(27))
     own = pack[12:15]
     total_t[...] = jnp.zeros_like(total_t)
     total_j[...] = jnp.zeros_like(total_j)
@@ -553,11 +562,14 @@
     phases(wave_tables(sizes, norm, waves, pack[12:15], wrow), wrow, *trig)
     wait()
     bufs = (got_t, got_j, part, got_rs, block, got_ar, got_ag, lhs, pot_s)
-    mine[...] = reciprocal(sizes, 0.0, sums_t, sums_j, base9, pack, refrow, pots, wrow, trig, bufs, sems)
+    sums = hand_sums(sizes, sums_t, got_t, sems[0], sems[1], LEVEL + APART)
+    mine[...], third = reciprocal(sizes, 0.0, sums, sums_t, sums_j, base9, pack, refrow, pots, wrow, trig, bufs, sems)
+    for c in third:
+        c.wait()
 
 
 def force_kernel(pots, mine, lists, pack, feats, gtab, mst, wz, wr, site, forces, mask, ranks, total):
-    rank_edges(lists, ranks, mask)
+    rank_edges(lists, ranks, mask, range(27))
     own = pack[12:15]
     total[...] = jnp.zeros_like(total)
 

time: 59.4 us -> 58.4 us (0.983)
  Pallas kernels: 55.3 us -> 54.3 us
    pallas_call x1, Pallas kernels: 55.3 us -> 54.3 us  [direct(): pl.pallas_call(functools.partial(whole_kernel, sizes, norm), out_shape=[s...]
where the time goes in v4:
time: 58.4 us; the launch traced here: 58.1 us
  Pallas kernels  54.3 us (93%)
  local copies, waits for them, and re-layouts  2.34 us (4%)
  between operations  1.47 us (3%)
    pallas_call x1, Pallas kernels, direct(): pl.pallas_call(functools.partial(whole_kernel, sizes, norm), out_shape=[s...  54.3 us
    unnamed x26, local copies, waits for them, and re-layouts  2.34 us

profile of v4, /device:TPU:1, one launch (start us, length us, event | category | flops | bytes accessed | tf_op | source)
XLA Modules:
  0.0 58.1 jit_solution(15191592118276327919)
XLA Ops:
  0.6 0.0 copy-start.3
  1.3 0.0 copy-start.6
  1.3 0.0 copy-start.9
  1.3 0.0 copy-start
  1.3 0.0 copy-done.3
  1.4 0.6 %copy-done.6 = f32[128,8]{0,1:T(8,128)S(1)} copy-done((f32[128,8]{0,1:T(8,128)S(1)}, f32[128,8]{0,1:T(8,128)}, u32[]{:S(2)}) %copy-start.6) | copy-done | bytes 4120
  2.0 0.0 copy-done.9
  2.0 0.0 copy-start.1
  2.0 0.0 copy-start.2
  2.0 0.0 copy-start.4
  2.0 0.0 copy-start.7
  2.0 0.0 copy-start.10
  2.0 0.0 copy-start.11
  2.0 54.3 %whole.1 = (f32[1,128]{1,0:T(1,128)S(1)}, f32[3,1,128]{2,1,0:T(1,128)S(1)}) custom-call(s32[12,1,128]{2,1,0:T(1,128)} %bitcast.17, s32[3,1,128]{2,1,0:T(1,128)} %bitcast.21, s32[1,1]{1,0:T(1,128)} %bitcast.14.counts, bf16[128,512]{1,0:T(8,128)(2,1)} %bitcast.15, s32[1,128]{1,0:T(1,128)S(1)} %bitcast.23, s32[3,2048]{1,0:T(4,128)} %rest_2_.1, ...), custom_call_target="tpu_custom_call" | custom-call | tf_op jit(solution)/shard_map/whole/pallas_call | solution.py:666
  56.3 0.0 copy-start.5
  56.3 0.0 copy-start.8
  56.4 0.0 copy-done
  56.4 0.0 copy-done.1
  56.4 0.0 copy-done.2
  56.4 0.0 copy-done.4
  56.4 0.0 copy-done.7
  56.4 0.0 copy-done.10
  56.4 0.0 copy-done.11
  56.4 0.6 copy-done.5
  57.0 0.0 copy-done.8
  57.0 0.5 copy.22
  57.5 0.6 copy.23
  (1 shorter events, 0.0 us)
Async XLA Ops:
  0.6 0.7 %copy-start.3 = (bf16[64,128]{1,0:T(8,128)(2,1)S(1)}, bf16[64,128]{1,0:T(8,128)(2,1)}, u32[]{:S(2)}) copy-start(bf16[64,128]{1,0:T(8,128)(2,1)} %rest_4_.1) | copy-start | bytes 49156
  1.3 0.7 %copy-start.6 = (f32[128,8]{0,1:T(8,128)S(1)}, f32[128,8]{0,1:T(8,128)}, u32[]{:S(2)}) copy-start(f32[128,8]{0,1:T(8,128)} %param.26) | copy-start | bytes 12292
  1.3 0.7 %copy-start.9 = (s32[1,1,1,128]{3,2,1,0:T(1,128)S(1)}, s32[1,1,1,128]{3,2,1,0:T(1,128)}, u32[]{:S(2)}) copy-start(s32[1,1,1,128]{3,2,1,0:T(1,128)} %param.17) | copy-start | bytes 1540
  1.3 55.1 %copy-start = (bf16[1,1,1,128,512]{4,3,2,1,0:T(8,128)(2,1)S(1)}, bf16[1,1,1,128,512]{4,3,2,1,0:T(8,128)(2,1)}, u32[]{:S(2)}) copy-start(bf16[1,1,1,128,512]{4,3,2,1,0:T(8,128)(2,1)} %param.15) | copy-start | bytes 393220
  2.0 54.4 %copy-start.1 = (bf16[128,128]{1,0:T(8,128)(2,1)S(1)}, bf16[128,128]{1,0:T(8,128)(2,1)}, u32[]{:S(2)}) copy-start(bf16[128,128]{1,0:T(8,128)(2,1)} %rest_6_.1) | copy-start | bytes 98308
  2.0 54.4 %copy-start.2 = (s32[3,2048]{1,0:T(4,128)S(1)}, s32[3,2048]{1,0:T(4,128)}, u32[]{:S(2)}) copy-start(s32[3,2048]{1,0:T(4,128)} %rest_2_.1) | copy-start | bytes 73732
  2.0 54.4 %copy-start.4 = (f32[10,128]{1,0:T(8,128)S(1)}, f32[10,128]{1,0:T(8,128)}, u32[]{:S(2)}) copy-start(f32[10,128]{1,0:T(8,128)} %rest_5_.1) | copy-start | bytes 15364
  2.0 54.4 %copy-start.7 = (bf16[8,64]{1,0:T(8,128)(2,1)S(1)}, bf16[8,64]{1,0:T(8,128)(2,1)}, u32[]{:S(2)}) copy-start(bf16[8,64]{1,0:T(8,128)(2,1)} %rest_3_.1) | copy-start | bytes 3076
  2.0 54.4 %copy-start.10 = (f32[128]{0:T(128)S(1)}, f32[128]{0:T(128)}, u32[]{:S(2)}) copy-start(f32[128]{0:T(128)} %param.25) | copy-start | bytes 1540
  2.0 54.4 %copy-start.11 = (f32[10]{0:T(128)S(1)}, f32[10]{0:T(128)}, u32[]{:S(2)}) copy-start(f32[10]{0:T(128)} %param.27) | copy-start | bytes 124
  56.3 0.7 %copy-start.5 = (s32[1,1,1,12,128]{4,2,3,1,0:T(1,128)S(1)}, s32[1,1,1,12,128]{4,2,3,1,0:T(1,128)}, u32[]{:S(2)}) copy-start(s32[1,1,1,12,128]{4,2,3,1,0:T(1,128)} %param.19) | copy-start | bytes 18436
  56.3 0.7 %copy-start.8 = (s32[1,1,1,3,128]{4,2,3,1,0:T(1,128)S(1)}, s32[1,1,1,3,128]{4,2,3,1,0:T(1,128)}, u32[]{:S(2)}) copy-start(s32[1,1,1,3,128]{4,2,3,1,0:T(1,128)} %param.16) | copy-start | bytes 4612

commit v5 on v4

--- a/solution.py
+++ b/solution.py
@@ -19,6 +19,7 @@
 GROUP = 9
 LOG2E = math.log2(math.e)
 FAR = -1.0e6
+ALL_VMEM = 67_043_328
 LIST = jnp.int16
 
 
@@ -67,6 +68,7 @@
 LEVEL = [i for i, d in enumerate(OFFS) if d[0] == 0]
 APART = [i for i, d in enumerate(OFFS) if d[0] != 0]
 NEAR = [(i, OFFS[i]) for i in LEVEL + APART if i != 13]
+NEAR.sort(key=lambda n: (n[0] in APART, -abs(n[1][1]) - abs(n[1][2])))
 
 
 SIDE = 128
@@ -299,10 +301,12 @@
 def peers(sizes):
     nx, ny, nz = sizes
     plane = [(dx, flip, dz) for dx in range(nx) for flip in range(2) for dz in range(nz)][1:]
-    line = [(0, dy, 0) for dy in range(2, ny, 2)]
+    plane.sort(key=lambda d: -min(d[0], nx - d[0]) - d[1] - min(d[2], nz - d[2]))
+    line = sorted([(0, dy, 0) for dy in range(2, ny, 2)], key=lambda d: -min(d[1], ny - d[1]))
     near = [d for _, d in NEAR]
     known = [((d[0] + nx) % nx, abs(d[1]), (d[2] + nz) % nz) for d in near]
-    whom = [at_offset(sizes, d) for d in near + line] + [in_plane(sizes, d) for d in plane if d not in known]
+    whom = [at_offset(sizes, d) for d in line] + [in_plane(sizes, d) for d in plane if d not in known]
+    whom += [at_offset(sizes, d) for d in near[::-1]]
     return plane, line, whom
 
 
@@ -622,7 +626,7 @@
         in_specs=[HBM, HBM, SMEM] + [VMEM] * 9,
         out_specs=[VMEM] * 8,
         scratch_shapes=[pltpu.VMEM((16, 128), jnp.int32), pltpu.VMEM((16, 128), LIST), dma((15,)), dma((27,)), dma((27,))],
-        compiler_params=pltpu.CompilerParams(collective_id=1, has_side_effects=True),
+        compiler_params=pltpu.CompilerParams(collective_id=1, has_side_effects=True, vmem_limit_bytes=ALL_VMEM),
         name="spread",
     )(neighbors, positions, counts, feats, species, *params)
     ranking = [pltpu.VMEM(*RANKS[1]), pltpu.VMEM(*RANKS[0])]
@@ -632,6 +636,7 @@
         in_specs=[VMEM] * 7,
         out_specs=[VMEM] * 2,
         scratch_shapes=ranking + [pltpu.VMEM((27, 16, 128), F32), pltpu.VMEM((27, 48, 128), F32)],
+        compiler_params=pltpu.CompilerParams(vmem_limit_bytes=ALL_VMEM),
         name="edges",
     )(lists, pack, feats, gtab, mst, wz, wr)
     bufs, sems = wave_buffers(sizes, waves.shape[1])
@@ -641,7 +646,7 @@
         in_specs=[VMEM] * 6,
         out_specs=[VMEM] * 2,
         scratch_shapes=bufs + sems,
-        compiler_params=pltpu.CompilerParams(collective_id=2, has_side_effects=True),
+        compiler_params=pltpu.CompilerParams(collective_id=2, has_side_effects=True, vmem_limit_bytes=ALL_VMEM),
         name="waves",
     )(sums_t, sums_j, base9, pack, waves, refrow)
     return pl.pallas_call(

time: 58.4 us -> 56.8 us (0.973)
  Pallas kernels: 54.3 us -> 53.5 us
    pallas_call x1, Pallas kernels: 54.3 us -> 53.5 us  [direct(): pl.pallas_call(functools.partial(whole_kernel, sizes, norm), out_shape=[s...]
    unnamed x26 -> x12, local copies, waits for them, and re-layouts: 2.34 us -> 1.76 us
where the time goes in v5:
time: 56.8 us; the launch traced here: 56.7 us
  Pallas kernels  53.5 us (94%)
  local copies, waits for them, and re-layouts  1.76 us (3%)
  between operations  1.39 us (2%)
    pallas_call x1, Pallas kernels, direct(): pl.pallas_call(functools.partial(whole_kernel, sizes, norm), out_shape=[s...  53.5 us
    unnamed x12, local copies, waits for them, and re-layouts  1.76 us

profile of v5, /device:TPU:1, one launch (start us, length us, event | category | flops | bytes accessed | tf_op | source)
XLA Modules:
  0.0 56.7 jit_solution(5958081837734064817)
XLA Ops:
  0.6 0.0 copy-start.6
  1.3 0.0 copy-start.4
  1.3 0.0 copy-start
  1.3 0.0 copy-start.2
  1.3 0.0 copy-start.8
  1.3 0.0 copy-done.6
  1.3 0.6 %copy-done.4 = f32[128,8]{0,1:T(8,128)S(1)} copy-done((f32[128,8]{0,1:T(8,128)S(1)}, f32[128,8]{0,1:T(8,128)}, u32[]{:S(2)}) %copy-start.4) | copy-done | bytes 4120
  2.0 0.0 copy-done
  2.0 0.0 copy-done.2
  2.0 0.0 copy-done.8
  2.0 53.5 %whole.1 = (f32[1,128]{1,0:T(1,128)S(1)}, f32[3,1,128]{2,1,0:T(1,128)S(1)}) custom-call(s32[12,1,128]{2,1,0:T(1,128)S(1)} %bitcast.17, s32[3,1,128]{2,1,0:T(1,128)} %bitcast.21, s32[1,1]{1,0:T(1,128)} %bitcast.14.counts, bf16[128,512]{1,0:T(8,128)(2,1)} %bitcast.15, s32[1,128]{1,0:T(1,128)S(1)} %bitcast.23, s32[3,2048]{1,0:T(4,128)} %rest_2_.1, ...), custom_call_target="tpu_custom_call" | custom-call | tf_op jit(solution)/shard_map/whole/pallas_call | solution.py:671
  55.6 0.5 copy.22
  56.1 0.6 copy.23
  (1 shorter events, 0.0 us)
Async XLA Ops:
  0.6 0.7 %copy-start.6 = (bf16[8,64]{1,0:T(8,128)(2,1)S(1)}, bf16[8,64]{1,0:T(8,128)(2,1)}, u32[]{:S(2)}) copy-start(bf16[8,64]{1,0:T(8,128)(2,1)} %rest_3_.1) | copy-start | bytes 3076
  1.3 0.7 %copy-start.4 = (f32[128,8]{0,1:T(8,128)S(1)}, f32[128,8]{0,1:T(8,128)}, u32[]{:S(2)}) copy-start(f32[128,8]{0,1:T(8,128)} %param.26) | copy-start | bytes 12292
  1.3 0.7 %copy-start = (f32[10,128]{1,0:T(8,128)S(1)}, f32[10,128]{1,0:T(8,128)}, u32[]{:S(2)}) copy-start(f32[10,128]{1,0:T(8,128)} %rest_5_.1) | copy-start | bytes 15364
  1.3 0.7 %copy-start.2 = (s32[1,1,1,12,128]{4,2,3,1,0:T(1,128)S(1)}, s32[1,1,1,12,128]{4,2,3,1,0:T(1,128)}, u32[]{:S(2)}) copy-start(s32[1,1,1,12,128]{4,2,3,1,0:T(1,128)} %param.19) | copy-start | bytes 18436
  1.3 0.7 %copy-start.8 = (s32[1,1,1,128]{3,2,1,0:T(1,128)S(1)}, s32[1,1,1,128]{3,2,1,0:T(1,128)}, u32[]{:S(2)}) copy-start(s32[1,1,1,128]{3,2,1,0:T(1,128)} %param.17) | copy-start | bytes 1540

commit v6 on v5

--- a/solution.py
+++ b/solution.py
@@ -40,14 +40,26 @@
     return hi, (x - hi.astype(F32)).astype(BF16)
 
 
+COORDS = {}
+
+
+def along(axis, size, o):
+    if (axis, o % size) not in COORDS:
+        here = lax.axis_index(axis)
+        COORDS[axis, o % size] = lax.rem(here + o % size, size) if o % size else here
+    return COORDS[axis, o % size]
+
+
 def at_offset(sizes, d):
-    return tuple(lax.rem(lax.axis_index(n) + (s + o), s) if o else lax.axis_index(n) for n, s, o in zip(AXES, sizes, d))
+    return tuple(along(n, s, o) for n, s, o in zip(AXES, sizes, d))
 
 
 def in_plane(sizes, d):
     dx, flip, dz = d
     x, y, z = at_offset(sizes, (dx, 0, dz))
-    return x, y + 1 - 2 * lax.rem(y, 2) if flip else y, z
+    if flip and "flip" not in COORDS:
+        COORDS["flip"] = y + 1 - 2 * lax.rem(y, 2)
+    return x, COORDS["flip"] if flip else y, z
 
 
 def greet(devices):
@@ -452,6 +464,7 @@
     cos_h, cos_l, sin_h, sin_l, got_t, got_j, part, got_rs, block, got_ar, got_ag, lhs, pot_s,
     psem, ls, lr, *sems,
 ):
+    COORDS.clear()
     wait = greet(peers(sizes)[2])
     packed = gather_pack(neighbors, positions, counts, pack, psem)
     brought = [pltpu.make_async_copy(f, n, osem.at[i]) for i, (f, n) in enumerate(zip(far, near))]
@@ -518,6 +531,7 @@
     sizes, neighbors, positions, counts, feats, species, rin, rout, gain, mix, readout, cw, ref_energy,
     lists, pack_out, gtab, mst, wz, wr, base9, refrow, pack, short, psem, ssem, rsem,
 ):
+    COORDS.clear()
     wait = greet([at_offset(sizes, d) for _, d in NEAR])
     packed = gather_pack(neighbors, positions, counts, pack, psem)
     tables(feats, species, rin, rout, gain, mix, readout, cw, ref_energy, gtab, mst, wz, wr, base9, refrow)
@@ -561,6 +575,7 @@
     sizes, norm, sums_t, sums_j, base9, pack, waves, refrow, pots, mine,
     wrow, cos_h, cos_l, sin_h, sin_l, got_t, got_j, part, got_rs, block, got_ar, got_ag, lhs, pot_s, *sems,
 ):
+    COORDS.clear()
     wait = greet(peers(sizes)[2])
     trig = (cos_h, cos_l, sin_h, sin_l)
     phases(wave_tables(sizes, norm, waves, pack[12:15], wrow), wrow, *trig)

time: 56.8 us -> 56.8 us (level)
  no operation moved by 1% of the time
where the time goes in v6:
time: 56.8 us; the launch traced here: 56.7 us
  Pallas kernels  53.5 us (94%)
  local copies, waits for them, and re-layouts  1.76 us (3%)
  between operations  1.39 us (2%)
    pallas_call x1, Pallas kernels, direct(): pl.pallas_call(functools.partial(whole_kernel, sizes, norm), out_shape=[s...  53.5 us
    unnamed x12, local copies, waits for them, and re-layouts  1.76 us

profile of v6, /device:TPU:1, one launch (start us, length us, event | category | flops | bytes accessed | tf_op | source)
XLA Modules:
  0.0 56.7 jit_solution(3814846973041890815)
XLA Ops:
  0.6 0.0 copy-start.6
  1.3 0.0 copy-start.4
  1.3 0.0 copy-start
  1.3 0.0 copy-start.2
  1.3 0.0 copy-start.8
  1.3 0.0 copy-done.6
  1.3 0.6 %copy-done.4 = f32[128,8]{0,1:T(8,128)S(1)} copy-done((f32[128,8]{0,1:T(8,128)S(1)}, f32[128,8]{0,1:T(8,128)}, u32[]{:S(2)}) %copy-start.4) | copy-done | bytes 4120
  2.0 0.0 copy-done
  2.0 0.0 copy-done.2
  2.0 0.0 copy-done.8
  2.0 53.5 %whole.1 = (f32[1,128]{1,0:T(1,128)S(1)}, f32[3,1,128]{2,1,0:T(1,128)S(1)}) custom-call(s32[12,1,128]{2,1,0:T(1,128)S(1)} %bitcast.17, s32[3,1,128]{2,1,0:T(1,128)} %bitcast.21, s32[1,1]{1,0:T(1,128)} %bitcast.14.counts, bf16[128,512]{1,0:T(8,128)(2,1)} %bitcast.15, s32[1,128]{1,0:T(1,128)S(1)} %bitcast.23, s32[3,2048]{1,0:T(4,128)} %rest_2_.1, ...), custom_call_target="tpu_custom_call" | custom-call | tf_op jit(solution)/shard_map/whole/pallas_call | solution.py:686
  55.6 0.5 copy.22
  56.1 0.6 copy.23
  (1 shorter events, 0.0 us)
Async XLA Ops:
  0.6 0.7 %copy-start.6 = (bf16[8,64]{1,0:T(8,128)(2,1)S(1)}, bf16[8,64]{1,0:T(8,128)(2,1)}, u32[]{:S(2)}) copy-start(bf16[8,64]{1,0:T(8,128)(2,1)} %rest_3_.1) | copy-start | bytes 3076
  1.3 0.7 %copy-start.4 = (f32[128,8]{0,1:T(8,128)S(1)}, f32[128,8]{0,1:T(8,128)}, u32[]{:S(2)}) copy-start(f32[128,8]{0,1:T(8,128)} %param.26) | copy-start | bytes 12292
  1.3 0.7 %copy-start = (f32[10,128]{1,0:T(8,128)S(1)}, f32[10,128]{1,0:T(8,128)}, u32[]{:S(2)}) copy-start(f32[10,128]{1,0:T(8,128)} %rest_5_.1) | copy-start | bytes 15364
  1.3 0.7 %copy-start.2 = (s32[1,1,1,12,128]{4,2,3,1,0:T(1,128)S(1)}, s32[1,1,1,12,128]{4,2,3,1,0:T(1,128)}, u32[]{:S(2)}) copy-start(s32[1,1,1,12,128]{4,2,3,1,0:T(1,128)} %param.19) | copy-start | bytes 18436
  1.3 0.7 %copy-start.8 = (s32[1,1,1,128]{3,2,1,0:T(1,128)S(1)}, s32[1,1,1,128]{3,2,1,0:T(1,128)}, u32[]{:S(2)}) copy-start(s32[1,1,1,128]{3,2,1,0:T(1,128)} %param.17) | copy-start | bytes 1540
